TPU v7x, 16 devices: a whole 2x2x2 slice. The times are simulated.
16 devices in a mesh: replica: 2 (over z), data: 8 (over y, x, core).
Axes of the slice: x: 2, y: 2, z: 2, core: 2. Of those that a mesh axis runs over, the one named last changes fastest.
Arguments:
- w_one: bfloat16 [4, 1280, 5120], replicated
- w_two: bfloat16 [4, 5120, 1280], replicated
- x_in: bfloat16 [48, 2, 128, 1280], P(('replica', 'data'))
- dy_in: bfloat16 [48, 2, 128, 1280], P(('replica', 'data'))
Outputs:
- output 1: bfloat16 [4, 1280, 5120], replicated
- output 2: bfloat16 [4, 5120, 1280], replicated
- output 3: bfloat16 [48, 2, 128, 1280], P(('replica', 'data'))
All inputs are finite; a program needn't handle non-finite values.
Results may differ from a plain program's by a relative error of at most 0.0160137.
Values are sent between devices in bfloat16 or wider.
A program may use at most 1 GiB of HBM per device.

v0:
```python
import jax
import jax.numpy as jnp
from jax import lax
from jax.sharding import PartitionSpec as P


def gelu_tanh(value):
    return jax.nn.gelu(value, approximate=True)


def forward_saved(w_one, w_two, tokens):
    layers = w_one.shape[0]
    saved_acts = []
    hidden = tokens
    for layer in range(layers):
        pre_act = jnp.dot(hidden, w_one[layer], preferred_element_type=jnp.float32).astype(jnp.bfloat16)
        gelu_out = gelu_tanh(pre_act.astype(jnp.float32)).astype(jnp.bfloat16)
        saved_acts.append((hidden, pre_act, gelu_out))
        if layer < layers - 1:
            hidden = (hidden.astype(jnp.float32) + jnp.dot(gelu_out, w_two[layer], preferred_element_type=jnp.float32)).astype(jnp.bfloat16)
    return saved_acts


def layer_backward(w_up, w_down, saved_layer, upstream):
    hidden, pre_act, gelu_out = saved_layer
    grad_b = upstream.astype(jnp.bfloat16)
    d_two = jnp.einsum("tf,tm->fm", gelu_out, grad_b, preferred_element_type=jnp.float32)
    d_act = jnp.einsum("tm,fm->tf", grad_b, w_down, preferred_element_type=jnp.float32)
    d_pre = jax.vjp(gelu_tanh, pre_act.astype(jnp.float32))[1](d_act)[0].astype(jnp.bfloat16)
    d_one = jnp.einsum("tm,tf->mf", hidden, d_pre, preferred_element_type=jnp.float32)
    new_upstream = upstream + jnp.einsum("tf,mf->tm", d_pre, w_up, preferred_element_type=jnp.float32)
    return d_one, d_two, new_upstream


def reduce_grads(accumulators):
    stacked = jnp.stack([part_acc.astype(jnp.bfloat16) for part_acc in accumulators])
    grad_shard = lax.psum_scatter(stacked, "data", scatter_dimension=1, tiled=True)
    grad_shard = lax.psum(grad_shard, "replica")
    return lax.all_gather(grad_shard, "data", axis=1, tiled=True)


def solution(mesh):
    batch_spec = P(("replica", "data"))

    def per_device(w_one, w_two, x_loc, dy_loc):
        micro_count, seq_count, length, model_width = x_loc.shape
        layers = w_one.shape[0]
        acc_one = [None] * layers
        acc_two = [None] * layers
        dx_parts = []
        for micro_idx in range(micro_count):
            saved_acts = forward_saved(w_one, w_two, x_loc[micro_idx].reshape(seq_count * length, model_width))
            upstream = dy_loc[micro_idx].reshape(seq_count * length, model_width).astype(jnp.float32)
            for layer in reversed(range(layers)):
                d_one, d_two, upstream = layer_backward(w_one[layer], w_two[layer], saved_acts[layer], upstream)
                if micro_idx > 0:
                    d_one = acc_one[layer] + d_one
                    d_two = acc_two[layer] + d_two
                acc_one[layer] = d_one
                acc_two[layer] = d_two
            dx_parts.append(upstream.astype(jnp.bfloat16).reshape(seq_count, length, model_width))
        return reduce_grads(acc_one), reduce_grads(acc_two), jnp.stack(dx_parts)

    return jax.shard_map(per_device, mesh=mesh, in_specs=(P(), P(), batch_spec, batch_spec), out_specs=(P(), P(), batch_spec), check_vma=False)
```

profile of v0, /device:TPU:0, one launch (start us, length us, event | category | flops | bytes accessed | tf_op | source)
XLA Modules:
  0.0 2421.8 jit_solution(5705297843197513756)
XLA Ops:
  18.5 10.3 fusion.424
  37.3 10.5 fusion.415
  56.5 10.3 fusion.406
  77.5 9.4 fusion.205
  86.9 10.4 fusion.380
  97.3 9.4 fusion.208
  106.7 9.6 fusion.362
  116.4 9.4 fusion.211
  125.8 9.5 fusion.344
  135.3 10.8 fusion.498
  154.5 10.3 fusion.427
  173.5 10.7 fusion.418
  192.9 10.3 fusion.409
  213.2 9.1 fusion.217
  222.3 9.5 fusion.377
  231.8 9.4 fusion.220
  241.2 9.7 fusion.359
  250.9 9.2 fusion.223
  260.2 8.8 fusion.341
  269.0 10.5 fusion.497
  279.5 11.0 fusion.500
  290.5 10.5 fusion.499
  301.0 11.2 fusion.502
  312.2 11.2 fusion.501
  323.3 10.1 fusion.214
  333.5 10.2 fusion.226
  352.2 10.3 fusion.421
  371.2 10.6 fusion.412
  390.4 10.3 fusion.403
  410.8 9.4 fusion.193
  420.2 10.4 fusion.383
  430.6 10.5 fusion.196
  441.1 9.4 fusion.365
  450.5 9.4 fusion.199
  468.3 9.4 fusion.202
  477.8 10.8 fusion.496
  488.6 10.5 fusion.495
  499.1 23.9 fusion.1
  523.0 23.7 fusion.2
  546.6 23.8 fusion.3
  570.5 22.5 fusion
  593.0 35.8 %pad_maximum_fusion = bf16[4,1280,5120]{1,2,0:T(8,128)(2,1)} fusion(bf16[1,1280,5120]{1,2,0:T(8,128)(2,1)} %fusion.3, bf16[1,1280,5120]{1,2,0:T(8,128)(2,1)} %fusion.2, bf16[1,1280,5120]{1,2,0:T(8,128)(2,1)} %fusion.1, bf16[1,1280,5120]{1,2,0:T(8,128)(2,1)} %fusion), kind=kLoop, calls=%fused_computation | loop fusion | flops 78643200 | bytes 104857600 | tf_op jit(solution)/shard_map/stack | solution.py:36
  628.8 86.6 %copy.26 = bf16[4,1280,5120]{2,0,1:T(4,128)(2,1)} copy(bf16[4,1280,5120]{1,2,0:T(8,128)(2,1)} %pad_maximum_fusion) | data formatting | bytes 104857600 | tf_op jit(solution)/shard_map/stack | solution.py:36
  717.1 13.1 fusion.445
  730.2 11.3 fusion.454
  741.5 11.2 fusion.448
  752.7 11.2 fusion.457
  763.9 11.4 fusion.451
  775.3 11.3 fusion.387
  786.6 11.9 fusion.389
  798.6 11.3 fusion.460
  809.9 26.8 %fusion.7 = bf16[1,5120,1280]{2,1,0:T(8,128)(2,1)} fusion(bf16[256,1280]{1,0:T(8,128)(2,1)S(1)} %bitcast.296, f32[5120,1280]{1,0:T(8,128)} %fusion.389, f32[5120,1280]{1,0:T(8,128)} %fusion.387, bf16[256,5120]{1,0:T(8,128)(2,1)} %copy-done.7), kind=kOutput, calls=%fused_computation.17 | convolution fusion | flops 3388211200 | bytes 68812800 | tf_op jit(solution)/shard_map/tf,tm->fm/dot_general | solution.py:27
  836.7 23.2 fusion.4
  859.9 24.6 %fusion.5 = bf16[1,5120,1280]{2,1,0:T(8,128)(2,1)} fusion(f32[5120,1280]{1,0:T(8,128)} %fusion.457, f32[5120,1280]{1,0:T(8,128)} %fusion.448, f32[256,1280]{1,0:T(8,128)} %copy-done.60, bf16[256,5120]{1,0:T(8,128)(2,1)} %copy-done.4), kind=kOutput, calls=%fused_computation.15 | convolution fusion | flops 3388538880 | bytes 69468160 | tf_op jit(solution)/shard_map/tf,tm->fm/dot_general | solution.py:27
  884.6 23.2 fusion.6
  907.8 35.8 %pad_maximum_fusion.1 = bf16[4,5120,1280]{2,1,0:T(8,128)(2,1)} fusion(bf16[1,5120,1280]{2,1,0:T(8,128)(2,1)} %fusion.7, bf16[1,5120,1280]{2,1,0:T(8,128)(2,1)} %fusion.6, bf16[1,5120,1280]{2,1,0:T(8,128)(2,1)} %fusion.5, bf16[1,5120,1280]{2,1,0:T(8,128)(2,1)} %fusion.4), kind=kLoop, calls=%fused_computation.1 | loop fusion | flops 78643200 | bytes 104857600 | tf_op jit(solution)/shard_map/stack | solution.py:36
  945.4 367.2 %all-reduce.5.cloned.1.call-done = bf16[4,1280,5120]{2,0,1:T(4,128)(2,1)} async-done(((bf16[4,1280,5120]{2,0,1:T(4,128)(2,1)}), bf16[4,1280,5120]{2,0,1:T(4,128)(2,1)}) %all-reduce.5.cloned.1.call-update) | async-done | bytes 52428816
  1320.5 282.7 %reduce-scatter.2.cloned.1.call-done = bf16[4,640,1280]{2,1,0:T(8,128)(2,1)} async-done(((bf16[4,5120,1280]{2,1,0:T(8,128)(2,1)}), bf16[4,640,1280]{2,1,0:T(8,128)(2,1)}) %reduce-scatter.2.cloned.1.call-update) | async-done | bytes 6553616 | tf_op jit(solution)/shard_map/reduce_scatter | solution.py:37
  1603.3 298.4 %all-reduce.7.cloned.1.call-done = (bf16[4,160,5120]{2,0,1:T(4,128)(2,1)}, bf16[4,640,1280]{2,1,0:T(8,128)(2,1)}) async-done(((bf16[4,160,5120]{2,0,1:T(4,128)(2,1)}, bf16[4,640,1280]{2,1,0:T(8,128)(2,1)}), (bf16[4,160,5120]{2,0,1:T(4,128)(2,1)}, bf16[4,640,1280]{2,1,0:T(8,128)(2,1)})) %all-reduce.7.cloned.1.call-update) | async-done | bytes 13107216 | tf_op jit(solution)/shard_map/psum | solution.py:38
  1903.4 8.8 fusion.433
  1930.7 209.9 %all-gather.3.cloned.1.call-done = bf16[4,1280,5120]{2,0,1:T(4,128)(2,1)} async-done(((bf16[4,160,5120]{2,0,1:T(4,128)(2,1)}), bf16[4,1280,5120]{2,0,1:T(4,128)(2,1)}) %all-gather.3.cloned.1.call-update) | async-done | bytes 52428816 | tf_op jit(solution)/shard_map/all_gather | solution.py:39
  2140.6 35.1 %copy.27 = bf16[4,1280,5120]{2,1,0:T(8,128)(2,1)} copy(bf16[4,1280,5120]{2,0,1:T(4,128)(2,1)} %all-gather.3.cloned.1.call-done) | data formatting | bytes 104857600
  2175.7 203.6 %all-gather.5.cloned.1.call-done = bf16[4,5120,1280]{2,1,0:T(8,128)(2,1)} async-done(((bf16[4,640,1280]{2,1,0:T(8,128)(2,1)}), bf16[4,5120,1280]{2,1,0:T(8,128)(2,1)}) %all-gather.5.cloned.1.call-update) | async-done | bytes 52428816 | tf_op jit(solution)/shard_map/all_gather | solution.py:39
  2379.4 35.4 %copy.41 = bf16[4,5120,1280]{2,1,0:T(8,128)(2,1)} copy(bf16[4,5120,1280]{2,1,0:T(8,128)(2,1)} %all-gather.5.cloned.1.call-done) | data formatting | bytes 104857600
  (178 shorter events, 149.9 us)
Async XLA Ops:
  7.2 1305.4 %all-reduce.5.cloned.1.call-start = ((), (), s32[]{:S(2)}) async-start(), calls=%async_computation.4 | async-start | bytes 104857600
  18.5 10.3 copy-start.24
  37.3 79.1 %copy-start.22 = (bf16[256,5120]{1,0:T(8,128)(2,1)}, bf16[256,5120]{1,0:T(8,128)(2,1)S(1)}, u32[]{:S(2)}) copy-start(bf16[256,5120]{1,0:T(8,128)(2,1)S(1)} %fusion.125) | copy-start | bytes 7864324
  56.5 40.8 %copy-start.20 = (bf16[256,5120]{1,0:T(8,128)(2,1)}, bf16[256,5120]{1,0:T(8,128)(2,1)S(1)}, u32[]{:S(2)}) copy-start(bf16[256,5120]{1,0:T(8,128)(2,1)S(1)} %fusion.134) | copy-start | bytes 7864324
  66.8 8.7 copy-start.65
  66.9 8.7 copy-start.48
  77.0 9.9 copy-start.42
  86.9 10.4 copy-start.34
  106.7 9.7 copy-start.36
  116.4 9.4 copy-start.55
  135.3 10.8 copy-start.44
  154.5 10.3 copy-start.31
  173.5 77.5 %copy-start.29 = (bf16[256,5120]{1,0:T(8,128)(2,1)}, bf16[256,5120]{1,0:T(8,128)(2,1)S(1)}, u32[]{:S(2)}) copy-start(bf16[256,5120]{1,0:T(8,128)(2,1)S(1)} %fusion.122) | copy-start | bytes 7864324
  192.9 38.9 %copy-start.27 = (bf16[256,5120]{1,0:T(8,128)(2,1)}, bf16[256,5120]{1,0:T(8,128)(2,1)S(1)}, u32[]{:S(2)}) copy-start(bf16[256,5120]{1,0:T(8,128)(2,1)S(1)} %fusion.131) | copy-start | bytes 7864324
  203.2 9.9 copy-start.40
  260.2 8.8 copy-start.72
  269.0 64.5 %copy-start.50 = (f32[256,1280]{1,0:T(8,128)}, f32[256,1280]{1,0:T(8,128)S(1)}, u32[]{:S(2)}) copy-start(f32[256,1280]{1,0:T(8,128)S(1)} %fusion.341) | copy-start | bytes 3932164
  269.0 10.5 copy-start.37
  269.0 10.5 copy-start.68
  279.5 11.0 copy-start.70
  290.5 10.5 copy-start.35
  290.5 10.5 copy-start.66
  312.2 11.2 copy-start.25
  312.2 11.2 copy-start.49
  323.3 10.1 copy-start.32
  333.5 10.2 copy-start.18
  352.1 116.1 %copy-start.5 = (bf16[256,5120]{1,0:T(8,128)(2,1)}, bf16[256,5120]{1,0:T(8,128)(2,1)S(1)}, u32[]{:S(2)}) copy-start(bf16[256,5120]{1,0:T(8,128)(2,1)S(1)} %fusion.119) | copy-start | bytes 7864324
  371.1 79.4 %copy-start.4 = (bf16[256,5120]{1,0:T(8,128)(2,1)}, bf16[256,5120]{1,0:T(8,128)(2,1)S(1)}, u32[]{:S(2)}) copy-start(bf16[256,5120]{1,0:T(8,128)(2,1)S(1)} %fusion.128) | copy-start | bytes 7864324
  390.4 40.3 %copy-start.2 = (bf16[256,5120]{1,0:T(8,128)(2,1)}, bf16[256,5120]{1,0:T(8,128)(2,1)S(1)}, u32[]{:S(2)}) copy-start(bf16[256,5120]{1,0:T(8,128)(2,1)S(1)} %fusion.137) | copy-start | bytes 7864324
  400.7 8.7 copy-start.61
  400.7 10.1 copy-start.16
  420.2 10.4 copy-start.38
  450.5 9.4 copy-start.60
  468.3 9.4 copy-start.58
  468.3 9.4 copy-start.14
  468.3 9.4 copy-start.47
  477.7 92.7 %copy-start = (bf16[256,5120]{1,0:T(8,128)(2,1)}, bf16[256,5120]{1,0:T(8,128)(2,1)S(1)}, u32[]{:S(2)}) copy-start(bf16[256,5120]{1,0:T(8,128)(2,1)S(1)} %fusion.202) | copy-start | bytes 7864324
  477.7 10.9 copy-start.12
  477.8 10.8 copy-start.45
  499.1 23.9 copy-start.63
  546.6 23.8 copy-start.19
  715.4 887.8 %reduce-scatter.2.cloned.1.call-start = ((), (), s32[]{:S(2)}) async-start(), calls=%async_computation.2 | async-start | bytes 58982400 | tf_op jit(solution)/shard_map/reduce_scatter | solution.py:37
  717.1 13.1 copy-start.33
  717.1 13.1 copy-start.51
  730.2 11.3 copy-start.23
  730.2 11.3 copy-start.56
  741.5 11.2 copy-start.30
  741.5 11.2 copy-start.57
  752.7 11.2 copy-start.21
  752.7 11.2 copy-start.53
  763.9 11.4 copy-start.9
  763.9 11.4 copy-start.43
  775.3 11.3 copy-start.11
  775.3 11.3 copy-start.41
  786.6 11.9 copy-start.28
  786.6 11.9 copy-start.54
  798.6 11.3 copy-start.17
  809.9 26.8 %copy-start.6 = (bf16[256,5120]{1,0:T(8,128)(2,1)S(1)}, bf16[256,5120]{1,0:T(8,128)(2,1)}, u32[]{:S(2)}) copy-start(bf16[256,5120]{1,0:T(8,128)(2,1)} %copy-done.5) | copy-start | bytes 7864324
  859.9 24.6 %copy-start.3 = (bf16[256,5120]{1,0:T(8,128)(2,1)S(1)}, bf16[256,5120]{1,0:T(8,128)(2,1)}, u32[]{:S(2)}) copy-start(bf16[256,5120]{1,0:T(8,128)(2,1)} %copy-done.2) | copy-start | bytes 7864324
  943.6 958.1 %all-reduce.7.cloned.1.call-start = ((), (), s32[]{:S(2)}) async-start(), calls=%async_computation.5 | async-start | bytes 26214400 | tf_op jit(solution)/shard_map/psum | solution.py:38
  1603.3 537.4 %all-gather.3.cloned.1.call-start = ((), (), s32[]{:S(2)}) async-start(), calls=%async_computation.1 | async-start | bytes 58982400 | tf_op jit(solution)/shard_map/all_gather | solution.py:39
  1901.7 477.7 %all-gather.5.cloned.1.call-start = ((), (), s32[]{:S(2)}) async-start(), calls=%async_computation.3 | async-start | bytes 58982400 | tf_op jit(solution)/shard_map/all_gather | solution.py:39
  1903.4 8.8 copy-start.13
  1903.4 8.8 copy-start.52
  (15 other events, 86.4 us)
Sparse Core Ops, SparseCore 0:
  715.5 597.0 all-reduce.4
  1316.8 286.3 reduce-scatter.1
  1606.3 295.3 all-reduce.6
  1903.4 237.1 all-gather.2
  2142.3 236.9 all-gather.4
where the time goes:
time: 2430 us; the launch traced here: 2420 us
  waiting for transfers between devices  1360 us (56%)
  matrix products  794 us (33%)
  local copies, waits for them, and re-layouts  177 us (7%)
  other arithmetic  73 us (3%)
    all_gather x2, waiting for transfers between devices, reduce_grads(): return lax.all_gather(grad_shard, 'data', axis=1, tiled=True)  414 us
    unnamed x6, waiting for transfers between devices  368 us
    psum x1, waiting for transfers between devices, reduce_grads(): grad_shard = lax.psum(grad_shard, 'replica')  298 us
    reduce_scatter x1, waiting for transfers between devices, reduce_grads(): lax.psum_scatter(stacked, 'data', scatter_dimension=1, tiled=True)  283 us
    dot_general x12, matrix products, layer_backward(): jnp.einsum('tf,tm->fm', gelu_out, grad_b, preferred_element_type=jnp.floa...  191 us
    dot_general x12, matrix products, layer_backward(): jnp.einsum('tm,tf->mf', hidden, d_pre, preferred_element_type=jnp.float32)  180 us
    dot_general x12, matrix products, layer_backward(): jnp.einsum('tm,fm->tf', grad_b, w_down, preferred_element_type=jnp.float32)  115 us
    dot_general x12, matrix products, layer_backward(): jnp.einsum('tf,mf->tm', d_pre, w_up, preferred_element_type=jnp.float32)  111 us
  transfers between devices with their start and end apart: 5, of which 5 were waited for; matrix products, arithmetic and copies ran while one was open for 12% of the time, Pallas kernels for 0%

commit v1 on v0

v1 whole, which is shorter than its diff:
```python
import functools

import jax
import jax.numpy as jnp
from jax import lax
from jax.experimental import pallas as pl
from jax.experimental.pallas import tpu as pltpu
from jax.sharding import PartitionSpec as P

AXES = ("replica", "data")


def gelu_tanh(value):
    return jax.nn.gelu(value, approximate=True)


def dot(lhs, rhs, lhs_dim, rhs_dim):
    return lax.dot_general(lhs, rhs, (((lhs_dim,), (rhs_dim,)), ((), ())), preferred_element_type=jnp.float32)


def place_body(piece_ref, *refs):
    refs[-1][0] = piece_ref[...]


def place(piece, stacked, layer, layers):
    rows, cols = piece.shape
    step = rows // 10
    spec = pl.BlockSpec((step, cols), lambda i: (i, 0))
    args, specs, alias = [piece], [spec], {}
    if stacked is not None:
        args.append(stacked)
        specs.append(pl.BlockSpec(memory_space=pl.ANY))
        alias = {1: 0}
    return pl.pallas_call(
        place_body,
        grid=(10,),
        out_shape=jax.ShapeDtypeStruct((layers, rows, cols), piece.dtype),
        in_specs=specs,
        out_specs=pl.BlockSpec((1, step, cols), lambda i: (layer, i, 0)),
        input_output_aliases=alias,
        cost_estimate=pl.CostEstimate(flops=rows * cols * 60, bytes_accessed=4 * rows * cols, transcendentals=0),
        name="place",
    )(*args)


def total(grad):
    shard = lax.psum_scatter(grad.astype(jnp.bfloat16), AXES, scatter_dimension=0, tiled=True)
    return lax.all_gather(shard, AXES, axis=0, tiled=True)


def solution(mesh):
    batch_spec = P(AXES)

    def per_device(w_one, w_two, x_loc, dy_loc):
        layers, width, _ = w_one.shape
        hidden = x_loc.reshape(-1, width)
        saved = []
        for layer in range(layers):
            pre_act = dot(hidden, w_one[layer], 1, 0).astype(jnp.bfloat16)
            act = gelu_tanh(pre_act.astype(jnp.float32)).astype(jnp.bfloat16)
            saved.append((hidden, pre_act, act))
            if layer < layers - 1:
                hidden = (hidden.astype(jnp.float32) + dot(act, w_two[layer], 1, 0)).astype(jnp.bfloat16)
        grad = dy_loc.reshape(-1, width).astype(jnp.float32)
        out_one = out_two = None
        for layer in reversed(range(layers)):
            hidden, pre_act, act = saved[layer]
            grad_b = grad.astype(jnp.bfloat16)
            t_two = total(dot(act, grad_b, 0, 0))
            d_act = dot(grad_b, w_two[layer], 1, 1)
            d_pre = jax.vjp(gelu_tanh, pre_act.astype(jnp.float32))[1](d_act)[0].astype(jnp.bfloat16)
            t_one = total(dot(hidden, d_pre, 0, 0))
            grad = grad + dot(d_pre, w_one[layer], 1, 1)
            out_two = place(t_two, out_two, layer, layers)
            out_one = place(t_one, out_one, layer, layers)
        return out_one, out_two, grad.astype(jnp.bfloat16).reshape(x_loc.shape)

    return jax.shard_map(per_device, mesh=mesh, in_specs=(P(), P(), batch_spec, batch_spec), out_specs=(P(), P(), batch_spec), check_vma=False)
```

time: 2430 us -> 1880 us (0.77)
  matrix products: 794 us -> 479 us
  local copies, waits for them, and re-layouts: 177 us -> 5.6 us
  Pallas kernels: 0 us -> 101 us
  waiting for transfers between devices: 1360 us -> 1280 us
  other arithmetic: 73 us -> 0 us
    reduce_scatter x1 -> x8, waiting for transfers between devices: 283 us -> 853 us  [total(): lax.psum_scatter(grad.astype(jnp.bfloat16), AXES, scatter_dimension=0, ti...]
    unnamed x6 -> x16, waiting for transfers between devices: 368 us -> 0.9 us
    dot_general x69 -> x23, matrix products: 794 us -> 479 us  [dot(): lax.dot_general(lhs, rhs, (((lhs_dim,), (rhs_dim,)), ((), ())), preferred...]
    psum x1 -> x0, waiting for transfers between devices: 298 us -> none  [reduce_grads(): grad_shard = lax.psum(grad_shard, 'replica')]
    pallas_call x0 -> x8, Pallas kernels: none -> 101 us  [place(): pl.pallas_call(place_body, grid=(10,), out_shape=jax.ShapeDtypeStruct((la...]
    another operation x1 -> x0, local copies, waits for them, and re-layouts: 86.6 us -> none  [reduce_grads(): jnp.stack([part_acc.astype(jnp.bfloat16) for part_acc in accumulators])]
    unnamed x152 -> x20, local copies, waits for them, and re-layouts: 86.1 us -> 5.6 us
    another operation x3 -> x0, other arithmetic: 73 us -> none  [the longest x2 71.5 us: reduce_grads(): jnp.stack([part_acc.astype(jnp.bfloat16) for part_acc in accumulators])]
  transfers between devices with their start and end apart: 5 -> 16, of which waited for: 5 -> 15; matrix products, arithmetic and copies ran while one was open for 12% -> 15% of each run, Pallas kernels for 0% -> 5%
where the time goes in v1:
time: 1880 us
  waiting for transfers between devices  1280 us (68%)
  matrix products  479 us (25%)
  Pallas kernels  101 us (5%)
    reduce_scatter x8, waiting for transfers between devices, total(): lax.psum_scatter(grad.astype(jnp.bfloat16), AXES, scatter_dimension=0, ti...  853 us
    dot_general x23, matrix products, dot(): lax.dot_general(lhs, rhs, (((lhs_dim,), (rhs_dim,)), ((), ())), preferred...  479 us
    all_gather x8, waiting for transfers between devices, total(): return lax.all_gather(shard, AXES, axis=0, tiled=True)  422 us
    pallas_call x8, Pallas kernels, place(): pl.pallas_call(place_body, grid=(10,), out_shape=jax.ShapeDtypeStruct((la...  101 us
  transfers between devices with their start and end apart: 16, of which 15 were waited for; matrix products, arithmetic and copies ran while one was open for 15% of the time, Pallas kernels for 5%

profile of v1, /device:TPU:0, one launch (start us, length us, event | category | flops | bytes accessed | tf_op | source)
XLA Modules:
  0.0 1876.3 jit_solution(13984590641079033730)
XLA Ops:
  7.2 0.0 reduce-scatter.23.cloned.1.call-start
  7.2 14.4 fusion.86
  21.7 21.2 %add_convert_fusion.3 = bf16[768,1280]{1,0:T(8,128)(2,1)S(1)} fusion(bf16[768,1280]{1,0:T(8,128)(2,1)S(1)} %bitcast.95, bf16[4,5120,1280]{2,1,0:T(8,128)(2,1)} %param.5, bf16[768,5120]{1,0:T(8,128)(2,1)S(1)} %fusion.86), kind=kOutput, calls=%fused_computation.125 | convolution fusion | flops 10108600320 | bytes 24903680 | tf_op jit(solution)/shard_map/dot_general | solution.py:18
  42.9 26.9 %fusion.89 = bf16[768,5120]{1,0:T(8,128)(2,1)} fusion(bf16[768,1280]{1,0:T(8,128)(2,1)S(1)} %add_convert_fusion.3, bf16[4,1280,5120]{2,1,0:T(8,128)(2,1)} %param.4), kind=kOutput, calls=%fused_computation.115 | convolution fusion | flops 10070261760 | bytes 22937600 | tf_op jit(solution)/shard_map/dot_general | solution.py:18
  69.8 20.6 %add_convert_fusion.2 = bf16[768,1280]{1,0:T(8,128)(2,1)S(1)} fusion(bf16[768,1280]{1,0:T(8,128)(2,1)S(1)} %add_convert_fusion.3, bf16[4,5120,1280]{2,1,0:T(8,128)(2,1)} %param.5, bf16[768,5120]{1,0:T(8,128)(2,1)} %fusion.89), kind=kOutput, calls=%fused_computation.124 | convolution fusion | flops 10108600320 | bytes 24903680 | tf_op jit(solution)/shard_map/dot_general | solution.py:18
  90.4 17.6 fusion.92
  108.0 20.7 %add_convert_fusion.1 = bf16[768,1280]{1,0:T(8,128)(2,1)} fusion(bf16[768,1280]{1,0:T(8,128)(2,1)S(1)} %add_convert_fusion.2, bf16[4,5120,1280]{2,1,0:T(8,128)(2,1)} %param.5, bf16[768,5120]{1,0:T(8,128)(2,1)} %fusion.92), kind=kOutput, calls=%fused_computation.123 | convolution fusion | flops 10108600320 | bytes 24903680 | tf_op jit(solution)/shard_map/dot_general | solution.py:18
  128.7 16.6 fusion.69
  145.4 28.3 %fusion.7 = (bf16[768,5120]{1,0:T(8,128)(2,1)}, bf16[768,5120]{1,0:T(8,128)(2,1)}) fusion(f32[768,5120]{1,0:T(8,128)} %fusion.69, bf16[768,1280]{1,0:T(8,128)(2,1)} %add_convert_fusion.1, bf16[4,1280,5120]{2,1,0:T(8,128)(2,1)} %param.4), kind=kOutput, calls=%fused_computation.35 | convolution fusion | flops 10152837120 | bytes 46530560 | tf_op jit(solution)/shard_map/dot_general | solution.py:18
  173.7 25.7 %convolution_convert_fusion = bf16[5120,1280]{1,0:T(8,128)(2,1)} fusion(bf16[768,1280]{1,0:T(8,128)(2,1)S(1)} %bitcast.92, bf16[768,5120]{1,0:T(8,128)(2,1)} %get-tuple-element.4), kind=kOutput, calls=%fused_computation.24 | convolution fusion | flops 10112204800 | bytes 22937600 | tf_op jit(solution)/shard_map/dot_general | solution.py:18
  199.4 0.0 reduce-scatter.15.cloned.1.call-start
  199.4 16.2 convolution_convert_fusion.4
  215.7 0.0 reduce-scatter.21.cloned.1.call-start
  215.7 15.3 convert_add_fusion.4
  231.1 1.9 copy-done.7
  233.0 25.7 %convolution_convert_fusion.1 = bf16[5120,1280]{1,0:T(8,128)(2,1)} fusion(f32[768,1280]{1,0:T(8,128)S(1)} %convert_add_fusion.4, bf16[768,5120]{1,0:T(8,128)(2,1)} %fusion.92), kind=kOutput, calls=%fused_computation.25 | convolution fusion | flops 10113187840 | bytes 24903680 | tf_op jit(solution)/shard_map/dot_general | solution.py:18
  258.7 0.0 reduce-scatter.19.cloned.1.call-start
  258.7 25.6 %fusion.10 = bf16[768,5120]{1,0:T(8,128)(2,1)} fusion(bf16[768,5120]{1,0:T(8,128)(2,1)} %fusion.92, bf16[4,5120,1280]{2,1,0:T(8,128)(2,1)} %param.5, f32[768,1280]{1,0:T(8,128)} %copy-done.7), kind=kOutput, calls=%fused_computation.38 | convolution fusion | flops 10149888000 | bytes 32768000 | tf_op jit(solution)/shard_map/dot_general | solution.py:18
  284.3 16.2 fusion.114
  300.6 1.9 copy-done.9
  302.4 25.8 %convolution_convert_fusion.2 = bf16[5120,1280]{1,0:T(8,128)(2,1)} fusion(f32[768,1280]{1,0:T(8,128)S(1)} %fusion.114, bf16[768,5120]{1,0:T(8,128)(2,1)} %fusion.89), kind=kOutput, calls=%fused_computation.26 | convolution fusion | flops 10113187840 | bytes 24903680 | tf_op jit(solution)/shard_map/dot_general | solution.py:18
  328.3 0.0 reduce-scatter.17.cloned.1.call-start
  328.3 26.0 %fusion.13 = bf16[768,5120]{1,0:T(8,128)(2,1)} fusion(bf16[768,5120]{1,0:T(8,128)(2,1)} %fusion.89, bf16[4,5120,1280]{2,1,0:T(8,128)(2,1)} %param.5, f32[768,1280]{1,0:T(8,128)} %copy-done.9), kind=kOutput, calls=%fused_computation.41 | convolution fusion | flops 10149888000 | bytes 32768000 | tf_op jit(solution)/shard_map/dot_general | solution.py:18
  354.3 16.2 fusion.111
  370.6 1.9 copy-done.8
  372.4 25.8 %convolution_convert_fusion.3 = bf16[5120,1280]{1,0:T(8,128)(2,1)} fusion(f32[768,1280]{1,0:T(8,128)S(1)} %fusion.111, bf16[768,5120]{1,0:T(8,128)(2,1)} %copy-done.6), kind=kOutput, calls=%fused_computation.27 | convolution fusion | flops 10113187840 | bytes 24903680 | tf_op jit(solution)/shard_map/dot_general | solution.py:18
  398.2 0.0 reduce-scatter.13.cloned.1.call-start
  398.3 16.5 convolution_convert_fusion.5
  414.8 0.0 reduce-scatter.11.cloned.1.call-start
  414.9 16.7 convolution_convert_fusion.6
  431.6 0.0 reduce-scatter.9.cloned.1.call-start
  431.7 26.1 %fusion.16 = bf16[768,5120]{1,0:T(8,128)(2,1)} fusion(bf16[768,5120]{1,0:T(8,128)(2,1)} %copy-done.6, bf16[4,5120,1280]{2,1,0:T(8,128)(2,1)} %param.5, f32[768,1280]{1,0:T(8,128)} %copy-done.8), kind=kOutput, calls=%fused_computation.44 | convolution fusion | flops 10149888000 | bytes 32768000 | tf_op jit(solution)/shard_map/dot_general | solution.py:18
  457.8 16.9 fusion.4
  474.7 0.0 all-gather.23.cloned.1.call-start
  474.8 0.7 all-gather.23.cloned.1.call-update
  475.5 0.0 all-gather.15.cloned.1.call-start
  475.5 8.0 reduce-scatter.15.cloned.1.call-done
  483.5 0.0 all-gather.21.cloned.1.call-start
  483.6 140.8 %reduce-scatter.21.cloned.1.call-done = bf16[320,1280]{1,0:T(8,128)(2,1)} async-done(((bf16[5120,1280]{1,0:T(8,128)(2,1)}), bf16[320,1280]{1,0:T(8,128)(2,1)}) %reduce-scatter.21.cloned.1.call-update) | async-done | bytes 819216 | tf_op jit(solution)/shard_map/reduce_scatter | solution.py:47
  624.4 0.0 all-gather.19.cloned.1.call-start
  624.4 140.6 %reduce-scatter.19.cloned.1.call-done = bf16[320,1280]{1,0:T(8,128)(2,1)} async-done(((bf16[5120,1280]{1,0:T(8,128)(2,1)}), bf16[320,1280]{1,0:T(8,128)(2,1)}) %reduce-scatter.19.cloned.1.call-update) | async-done | bytes 819216 | tf_op jit(solution)/shard_map/reduce_scatter | solution.py:47
  765.1 0.0 all-gather.17.cloned.1.call-start
  765.1 140.6 %reduce-scatter.17.cloned.1.call-done = bf16[320,1280]{1,0:T(8,128)(2,1)} async-done(((bf16[5120,1280]{1,0:T(8,128)(2,1)}), bf16[320,1280]{1,0:T(8,128)(2,1)}) %reduce-scatter.17.cloned.1.call-update) | async-done | bytes 819216 | tf_op jit(solution)/shard_map/reduce_scatter | solution.py:47
  905.8 140.6 %reduce-scatter.13.cloned.1.call-done = bf16[80,5120]{1,0:T(8,128)(2,1)} async-done(((bf16[1280,5120]{1,0:T(8,128)(2,1)}), bf16[80,5120]{1,0:T(8,128)(2,1)}) %reduce-scatter.13.cloned.1.call-update) | async-done | bytes 819216 | tf_op jit(solution)/shard_map/reduce_scatter | solution.py:47
  1046.5 141.3 %reduce-scatter.11.cloned.1.call-done = bf16[80,5120]{1,0:T(8,128)(2,1)} async-done(((bf16[1280,5120]{1,0:T(8,128)(2,1)}), bf16[80,5120]{1,0:T(8,128)(2,1)}) %reduce-scatter.11.cloned.1.call-update) | async-done | bytes 819216 | tf_op jit(solution)/shard_map/reduce_scatter | solution.py:47
  1187.8 0.0 all-gather.9.cloned.1.call-start
  1187.9 141.3 %reduce-scatter.9.cloned.1.call-done = bf16[80,5120]{1,0:T(8,128)(2,1)} async-done(((bf16[1280,5120]{1,0:T(8,128)(2,1)}), bf16[80,5120]{1,0:T(8,128)(2,1)}) %reduce-scatter.9.cloned.1.call-update) | async-done | bytes 819216 | tf_op jit(solution)/shard_map/reduce_scatter | solution.py:47
  1329.2 17.6 add_convert_fusion
  1346.8 46.9 %all-gather.23.cloned.1.call-done.piece_ref = bf16[5120,1280]{1,0:T(8,128)(2,1)} async-done(((bf16[320,1280]{1,0:T(8,128)(2,1)}), bf16[5120,1280]{1,0:T(8,128)(2,1)}) %all-gather.23.cloned.1.call-update) | async-done | bytes 13107216 | tf_op jit(solution)/shard_map/all_gather | solution.py:48
  1393.7 12.6 place.12.refs_0_
  1406.3 53.6 %all-gather.15.cloned.1.call-done.piece_ref = bf16[1280,5120]{1,0:T(8,128)(2,1)} async-done(((bf16[80,5120]{1,0:T(8,128)(2,1)}), bf16[1280,5120]{1,0:T(8,128)(2,1)}) %all-gather.15.cloned.1.call-update) | async-done | bytes 13107216 | tf_op jit(solution)/shard_map/all_gather | solution.py:48
  1459.8 12.6 place.8.refs_0_
  1472.4 53.7 %all-gather.21.cloned.1.call-done.piece_ref = bf16[5120,1280]{1,0:T(8,128)(2,1)} async-done(((bf16[320,1280]{1,0:T(8,128)(2,1)}), bf16[5120,1280]{1,0:T(8,128)(2,1)}) %all-gather.21.cloned.1.call-update) | async-done | bytes 13107216 | tf_op jit(solution)/shard_map/all_gather | solution.py:48
  1526.2 12.6 place.13.refs_0_
  1538.7 53.6 %all-gather.19.cloned.1.call-done.piece_ref = bf16[5120,1280]{1,0:T(8,128)(2,1)} async-done(((bf16[320,1280]{1,0:T(8,128)(2,1)}), bf16[5120,1280]{1,0:T(8,128)(2,1)}) %all-gather.19.cloned.1.call-update) | async-done | bytes 13107216 | tf_op jit(solution)/shard_map/all_gather | solution.py:48
  1592.3 12.6 place.14.refs_0_
  1604.9 53.7 %all-gather.17.cloned.1.call-done.piece_ref = bf16[5120,1280]{1,0:T(8,128)(2,1)} async-done(((bf16[320,1280]{1,0:T(8,128)(2,1)}), bf16[5120,1280]{1,0:T(8,128)(2,1)}) %all-gather.17.cloned.1.call-update) | async-done | bytes 13107216 | tf_op jit(solution)/shard_map/all_gather | solution.py:48
  1658.6 12.6 place.15
  1671.2 53.6 %all-gather.13.cloned.1.call-done.piece_ref = bf16[1280,5120]{1,0:T(8,128)(2,1)} async-done(((bf16[80,5120]{1,0:T(8,128)(2,1)}), bf16[1280,5120]{1,0:T(8,128)(2,1)}) %all-gather.13.cloned.1.call-update) | async-done | bytes 13107216 | tf_op jit(solution)/shard_map/all_gather | solution.py:48
  1724.8 12.6 place.9.refs_0_
  1737.3 53.6 %all-gather.11.cloned.1.call-done.piece_ref = bf16[1280,5120]{1,0:T(8,128)(2,1)} async-done(((bf16[80,5120]{1,0:T(8,128)(2,1)}), bf16[1280,5120]{1,0:T(8,128)(2,1)}) %all-gather.11.cloned.1.call-update) | async-done | bytes 13107216 | tf_op jit(solution)/shard_map/all_gather | solution.py:48
  1790.9 12.6 place.10.refs_0_
  1803.5 53.6 %all-gather.9.cloned.1.call-done.piece_ref = bf16[1280,5120]{1,0:T(8,128)(2,1)} async-done(((bf16[80,5120]{1,0:T(8,128)(2,1)}), bf16[1280,5120]{1,0:T(8,128)(2,1)}) %all-gather.9.cloned.1.call-update) | async-done | bytes 13107216 | tf_op jit(solution)/shard_map/all_gather | solution.py:48
  1857.0 12.6 place.11
  (35 shorter events, 0.4 us)
Async XLA Ops:
  7.2 467.6 %reduce-scatter.23.cloned.1.call-start = ((), (), s32[]{:S(2)}) async-start(), calls=%async_computation.22 | async-start | bytes 13926400 | tf_op jit(solution)/shard_map/reduce_scatter | solution.py:47
  7.2 14.5 copy-start.1
  21.7 21.2 %copy-start.6 = (bf16[768,5120]{1,0:T(8,128)(2,1)}, bf16[768,5120]{1,0:T(8,128)(2,1)S(1)}, u32[]{:S(2)}) copy-start(bf16[768,5120]{1,0:T(8,128)(2,1)S(1)} %fusion.86) | copy-start | bytes 23592964
  42.9 26.9 %copy-start.3 = (bf16[768,1280]{1,0:T(8,128)(2,1)}, bf16[768,1280]{1,0:T(8,128)(2,1)S(1)}, u32[]{:S(2)}) copy-start(bf16[768,1280]{1,0:T(8,128)(2,1)S(1)} %add_convert_fusion.3) | copy-start | bytes 5898244
  90.4 17.6 copy-start.5
  108.0 20.7 %copy-start = (bf16[3,2,128,1280]{3,2,1,0:T(8,128)(2,1)S(1)}, bf16[3,2,128,1280]{3,2,1,0:T(8,128)(2,1)}, u32[]{:S(2)}) copy-start(bf16[3,2,128,1280]{3,2,1,0:T(8,128)(2,1)} %param.7) | copy-start | bytes 5898244
  199.4 284.1 %reduce-scatter.15.cloned.1.call-start = ((), (), s32[]{:S(2)}) async-start(), calls=%async_computation.14 | async-start | bytes 13926400 | tf_op jit(solution)/shard_map/reduce_scatter | solution.py:47
  215.7 408.7 %reduce-scatter.21.cloned.1.call-start = ((), (), s32[]{:S(2)}) async-start(), calls=%async_computation.20 | async-start | bytes 13926400 | tf_op jit(solution)/shard_map/reduce_scatter | solution.py:47
  231.1 1.9 copy-start.7
  258.7 506.4 %reduce-scatter.19.cloned.1.call-start = ((), (), s32[]{:S(2)}) async-start(), calls=%async_computation.18 | async-start | bytes 13926400 | tf_op jit(solution)/shard_map/reduce_scatter | solution.py:47
  300.6 1.9 copy-start.9
  328.3 577.4 %reduce-scatter.17.cloned.1.call-start = ((), (), s32[]{:S(2)}) async-start(), calls=%async_computation.16 | async-start | bytes 13926400 | tf_op jit(solution)/shard_map/reduce_scatter | solution.py:47
  370.5 1.9 copy-start.8
  398.2 16.7 copy-start.4
  398.2 648.2 %reduce-scatter.13.cloned.1.call-start = ((), (), s32[]{:S(2)}) async-start(), calls=%async_computation.12 | async-start | bytes 13926400 | tf_op jit(solution)/shard_map/reduce_scatter | solution.py:47
  414.8 773.0 %reduce-scatter.11.cloned.1.call-start = ((), (), s32[]{:S(2)}) async-start(), calls=%async_computation.10 | async-start | bytes 13926400 | tf_op jit(solution)/shard_map/reduce_scatter | solution.py:47
  431.6 26.2 %copy-start.2 = (bf16[3,2,128,1280]{3,2,1,0:T(8,128)(2,1)S(1)}, bf16[3,2,128,1280]{3,2,1,0:T(8,128)(2,1)}, u32[]{:S(2)}) copy-start(bf16[3,2,128,1280]{3,2,1,0:T(8,128)(2,1)} %param.6) | copy-start | bytes 5898244
  431.6 897.6 %reduce-scatter.9.cloned.1.call-start = ((), (), s32[]{:S(2)}) async-start(), calls=%async_computation.8 | async-start | bytes 13926400 | tf_op jit(solution)/shard_map/reduce_scatter | solution.py:47
  474.7 919.0 %all-gather.23.cloned.1.call-start = ((), (), s32[]{:S(2)}) async-start(), calls=%async_computation.23 | async-start | bytes 13926400 | tf_op jit(solution)/shard_map/all_gather | solution.py:48
  475.5 984.4 %all-gather.15.cloned.1.call-start = ((), (), s32[]{:S(2)}) async-start(), calls=%async_computation.15 | async-start | bytes 13926400 | tf_op jit(solution)/shard_map/all_gather | solution.py:48
  483.5 1042.6 %all-gather.21.cloned.1.call-start = ((), (), s32[]{:S(2)}) async-start(), calls=%async_computation.21 | async-start | bytes 13926400 | tf_op jit(solution)/shard_map/all_gather | solution.py:48
  624.4 967.9 %all-gather.19.cloned.1.call-start = ((), (), s32[]{:S(2)}) async-start(), calls=%async_computation.19 | async-start | bytes 13926400 | tf_op jit(solution)/shard_map/all_gather | solution.py:48
  765.1 893.5 %all-gather.17.cloned.1.call-start = ((), (), s32[]{:S(2)}) async-start(), calls=%async_computation.17 | async-start | bytes 13926400 | tf_op jit(solution)/shard_map/all_gather | solution.py:48
  905.7 819.0 %all-gather.13.cloned.1.call-start = ((), (), s32[]{:S(2)}) async-start(), calls=%async_computation.13 | async-start | bytes 13926400 | tf_op jit(solution)/shard_map/all_gather | solution.py:48
  1046.4 744.5 %all-gather.11.cloned.1.call-start = ((), (), s32[]{:S(2)}) async-start(), calls=%async_computation.11 | async-start | bytes 13926400 | tf_op jit(solution)/shard_map/all_gather | solution.py:48
  1187.8 669.2 %all-gather.9.cloned.1.call-start = ((), (), s32[]{:S(2)}) async-start(), calls=%async_computation.9 | async-start | bytes 13926400 | tf_op jit(solution)/shard_map/all_gather | solution.py:48
Sparse Core Ops, SparseCore 0:
  199.5 143.1 reduce-scatter.22
  345.0 138.4 reduce-scatter.14
  485.8 138.4 reduce-scatter.20
  626.5 138.4 reduce-scatter.18
  767.2 138.4 reduce-scatter.16
  907.9 138.4 reduce-scatter.12
  1049.3 138.4 reduce-scatter.10
  1190.7 138.4 reduce-scatter.8
  1331.4 62.2 all-gather.22
  1395.8 64.0 all-gather.14
  1462.1 64.0 all-gather.20
  1528.2 64.0 all-gather.18
  1594.5 64.0 all-gather.16
  1660.7 64.0 all-gather.12
  1726.8 64.0 all-gather.10
  1793.0 64.0 all-gather.8

commit v2 on v1

v2 whole, which is shorter than its diff:
```python
import functools

import jax
import jax.numpy as jnp
from jax import lax
from jax.experimental import pallas as pl
from jax.experimental.pallas import tpu as pltpu
from jax.sharding import PartitionSpec as P

AXES = ("replica", "data")
MESH = pl.DeviceIdType.MESH
BF16, F32 = jnp.bfloat16, jnp.float32
VMEM_LIMIT = 67_043_328
C0, C1 = 0.7978845608028654, 0.044715
UNIT_ROWS = 256
SLOTS, RECV, LAG = 9, 6, 2


def gelu(v):
    return 0.5 * v * (1.0 + jnp.tanh(C0 * (v + C1 * (v * v * v))))


def gelu_slope(v):
    sq = v * v
    t = jnp.tanh(C0 * (v + C1 * (sq * v)))
    return 0.5 * (1.0 + t) + 0.5 * v * (1.0 - t * t) * (C0 * (1.0 + 3.0 * C1 * sq))


def mm(lhs, rhs, lhs_dim, rhs_dim):
    return lax.dot_general(lhs, rhs, (((lhs_dim,), (rhs_dim,)), ((), ())), preferred_element_type=F32)


def forward_body(x_ref, w1_ref, w2_ref, u_ref, a_ref, h_ref, hid, acc, *, layers, chunks):
    layer, j = pl.program_id(0), pl.program_id(1)

    @pl.when(jnp.logical_and(layer == 0, j == 0))
    def _():
        hid[...] = x_ref[...]

    @pl.when(j == 0)
    def _():
        h_ref[0] = hid[...]
        acc[...] = hid[...].astype(F32)

    pre = mm(hid[...], w1_ref[0], 1, 0).astype(BF16)
    u_ref[0] = pre
    act = gelu(pre.astype(F32)).astype(BF16)
    a_ref[0] = act

    @pl.when(layer < layers - 1)
    def _():
        acc[...] += mm(act, w2_ref[0], 1, 0)

        @pl.when(j == chunks - 1)
        def _():
            hid[...] = acc[...].astype(BF16)


def forward(x, w_one, w_two):
    layers, width, wide = w_one.shape
    tokens = x.shape[0]
    chunk = width
    chunks = wide // chunk
    act = jax.ShapeDtypeStruct((layers, tokens, wide), BF16)
    return pl.pallas_call(
        functools.partial(forward_body, layers=layers, chunks=chunks),
        grid=(layers, chunks),
        out_shape=[act, act, jax.ShapeDtypeStruct((layers, tokens, width), BF16)],
        in_specs=[
            pl.BlockSpec((tokens, width), lambda l, j: (0, 0)),
            pl.BlockSpec((1, width, chunk), lambda l, j: (l, 0, j)),
            pl.BlockSpec((1, chunk, width), lambda l, j: (l, j, 0)),
        ],
        out_specs=[
            pl.BlockSpec((1, tokens, chunk), lambda l, j: (l, 0, j)),
            pl.BlockSpec((1, tokens, chunk), lambda l, j: (l, 0, j)),
            pl.BlockSpec((1, tokens, width), lambda l, j: (l, 0, 0)),
        ],
        scratch_shapes=[pltpu.VMEM((tokens, width), BF16), pltpu.VMEM((tokens, width), F32)],
        compiler_params=pltpu.CompilerParams(vmem_limit_bytes=VMEM_LIMIT),
        name="forward",
    )(x, w_one, w_two)


def backward_body(
    w1, w2, u, a, h, dy,
    tot, dx, a_sib, h_sib, du_sib, gb_sib,
    a_cat, du_cat, h_cat, gb_cat, g, w2c, w1c, uc, du_st, unit, rcv1, rcv2, rcv3,
    s_rs1, s_rs2, s_rs3, s_ag1, s_ag2, s_ag3, s_fwd, s_own,
    r_rs1, r_rs2, r_rs3, r_ag1, r_ag2, r_ag3, r_fwd,
    c_rs1, c_rs2, c_rs3,
    s_a, r_a, l_a, l_a2, s_du, r_du, l_du, s_gb, r_gb, l_gb, l_gb2, s_h, r_h, l_h, l_h2, l_w2, l_w1, l_u, l_dx,
    *, layers, tokens, width, wide, rows,
):
    half = wide // 2
    nu = half // rows
    nm = width // rows
    hn = nu // 2
    chunk = wide // nu
    units = 2 * nu * layers
    z, rest = lax.axis_index("replica"), lax.axis_index("data")
    core, x, y = rest % 2, (rest // 2) % 2, rest // 4

    def pick(axis):
        return (1 - axis) * (2 - axis) // 2, axis * (2 - axis), axis * (axis - 1) // 2

    def bit(axis):
        ex, ey, ez = pick(axis)
        return ex * x + ey * y + ez * z

    def peer(axis):
        ex, ey, ez = pick(axis)
        px, py, pz = x + ex * (1 - 2 * x), y + ey * (1 - 2 * y), z + ez * (1 - 2 * z)
        return (pz, (py * 2 + px) * 2 + core)

    sibling = (z, (y * 2 + x) * 2 + 1 - core)

    def send(src, dst, ssem, rsem, to):
        return pltpu.make_async_remote_copy(src_ref=src, dst_ref=dst, send_sem=ssem, recv_sem=rsem, device_id=to, device_id_type=MESH)

    def place(n):
        p, q, r = n % 3, (n + 1) % 3, (n + 2) % 3
        k1 = 4 * bit(p)
        k2 = k1 + 2 * bit(q)
        return p, q, r, k1, k2, k2 + bit(r)

    def rs1(n):
        p, q, r, k1, k2, own = place(n)
        return send(unit.at[n % SLOTS, pl.ds(4 - k1, 4)], rcv1.at[n % RECV], s_rs1.at[n % SLOTS], r_rs1.at[n % RECV], peer(p))

    def rs2(n):
        p, q, r, k1, k2, own = place(n)
        return send(unit.at[n % SLOTS, pl.ds(k1 + 2 - (k2 - k1), 2)], rcv2.at[n % RECV], s_rs2.at[n % SLOTS], r_rs2.at[n % RECV], peer(q))

    def rs3(n):
        p, q, r, k1, k2, own = place(n)
        return send(unit.at[n % SLOTS, pl.ds(k2 + 1 - (own - k2), 1)], rcv3.at[n % RECV], s_rs3.at[n % SLOTS], r_rs3.at[n % RECV], peer(r))

    def own_copy(n):
        own = place(n)[5]
        return pltpu.make_async_copy(unit.at[n % SLOTS, pl.ds(own, 1)], tot.at[n, core, pl.ds(own, 1)], s_own.at[n % SLOTS])

    def ag1(n):
        p, q, r, k1, k2, own = place(n)
        return send(unit.at[n % SLOTS, pl.ds(own, 1)], tot.at[n, core, pl.ds(own, 1)], s_ag1.at[n % SLOTS], r_ag1.at[n % SLOTS], peer(r))

    def ag2(n):
        p, q, r, k1, k2, own = place(n)
        part = tot.at[n, core, pl.ds(k2, 2)]
        return send(part, part, s_ag2.at[n % SLOTS], r_ag2.at[n % SLOTS], peer(q))

    def ag3(n):
        p, q, r, k1, k2, own = place(n)
        part = tot.at[n, core, pl.ds(k1, 4)]
        return send(part, part, s_ag3.at[n % SLOTS], r_ag3.at[n % SLOTS], peer(p))

    def fwd(n):
        part = tot.at[n, core]
        return send(part, part, s_fwd.at[n % SLOTS], r_fwd.at[n % SLOTS], sibling)

    def add(n, block, rcv, j):
        slot = n % SLOTS
        unit[slot, block] = (unit[slot, block].astype(F32) + rcv[n % RECV, j].astype(F32)).astype(BF16)

    def credit(sem, n, axis):
        @pl.when(n + RECV < units)
        def _():
            pl.semaphore_signal(sem.at[n % RECV], inc=1, device_id=peer(axis), device_id_type=MESH)

    def spend(sem, n):
        @pl.when(n >= RECV)
        def _():
            pl.semaphore_wait(sem.at[n % RECV], 1)

    def live(n):
        return jnp.logical_and(n >= 0, n < units)

    def comm(t):
        n1, n2, n3, n4, n5, n6, n7 = (t - k * LAG for k in range(1, 8))

        @pl.when(live(n3))
        def _():
            p, q, r, k1, k2, own = place(n3)
            rs3(n3).wait_recv()
            add(n3, own, rcv3, 0)
            credit(c_rs3, n3, r)
            rs2(n3).wait_send()

        @pl.when(live(n2))
        def _():
            p, q, r, k1, k2, own = place(n2)
            rs2(n2).wait_recv()
            add(n2, k2 + 1 - (own - k2), rcv2, 1 - (own - k2))
            add(n2, own, rcv2, own - k2)
            credit(c_rs2, n2, q)
            rs1(n2).wait_send()

        @pl.when(live(n1))
        def _():
            p, q, r, k1, k2, own = place(n1)
            rs1(n1).wait_recv()
            keep = k2 - k1
            for j in range(2):
                add(n1, k1 + 2 - keep + j, rcv1, 2 - keep + j)
            for j in range(2):
                add(n1, k2 + j, rcv1, keep + j)
            credit(c_rs1, n1, p)

        @pl.when(live(n3))
        def _():
            own_copy(n3).start()
            ag1(n3).start()

        @pl.when(live(n2))
        def _():
            spend(c_rs3, n2)
            rs3(n2).start()

        @pl.when(live(n1))
        def _():
            spend(c_rs2, n1)
            rs2(n1).start()

        @pl.when(live(n4))
        def _():
            rs3(n4).wait_send()
            own_copy(n4).wait()
            ag1(n4).wait()
            ag2(n4).start()

        @pl.when(live(n5))
        def _():
            ag2(n5).wait()
            ag3(n5).start()

        @pl.when(live(n6))
        def _():
            ag3(n6).wait()
            fwd(n6).start()

        @pl.when(live(n7))
        def _():
            fwd(n7).wait()

    def push_unit(t):
        spend(c_rs1, t)
        rs1(t).start()

    def chunk_at(i):
        mine = i // hn
        return pl.multiple_of(((1 - core) + mine * (2 * core - 1)) * half + (i % hn) * chunk, 128)

    def loads(layer, i, slot):
        f0 = chunk_at(i)
        return (
            pltpu.make_async_copy(w2.at[layer, pl.ds(f0, chunk)], w2c.at[slot], l_w2.at[slot]),
            pltpu.make_async_copy(w1.at[layer, :, pl.ds(f0, chunk)], w1c.at[slot], l_w1.at[slot]),
            pltpu.make_async_copy(u.at[layer, :, pl.ds(f0, chunk)], uc.at[slot], l_u.at[slot]),
        )

    def cols(i):
        return pl.ds(pl.multiple_of(i * rows, 128), rows)

    def a_half(layer, i, which):
        return a.at[layer, :, pl.ds(pl.multiple_of(which * half + i * rows, 128), rows)]

    def a_load(layer, i):
        return pltpu.make_async_copy(a_half(layer, i, core), a_cat.at[pl.ds(0, tokens), cols(i)], l_a.at[i])

    def a_load2(layer, i):
        return pltpu.make_async_copy(a_sib.at[layer, :, cols(i)], a_cat.at[pl.ds(tokens, tokens), cols(i)], l_a2.at[i])

    def a_first(i):
        return send(a_half(layers - 1, i, 1 - core), a_cat.at[pl.ds(tokens, tokens), cols(i)], s_a.at[i], l_a2.at[i], sibling)

    def a_push(layer, i):
        return send(a_half(layer, i, 1 - core), a_sib.at[layer, :, cols(i)], s_a.at[i], r_a.at[layer % 2, i], sibling)

    def du_cols(i):
        return pl.ds(pl.multiple_of((i % hn) * chunk, 128), chunk)

    def du_push(layer, i):
        return send(du_st.at[i % 2], du_sib.at[layer, :, du_cols(i)], s_du.at[i % hn], r_du.at[i % hn], sibling)

    def du_load(layer, i):
        return pltpu.make_async_copy(du_sib.at[layer, :, du_cols(i)], du_cat.at[pl.ds(tokens, tokens), du_cols(i)], l_du.at[i % hn])

    own_rows, sib_rows = pl.ds(0, tokens), pl.ds(tokens, tokens)

    def h_push(layer):
        return send(h.at[layer], h_sib.at[layer], s_h, r_h, sibling)

    def h_load(layer):
        return pltpu.make_async_copy(h.at[layer], h_cat.at[own_rows], l_h)

    def h_load2(layer):
        return pltpu.make_async_copy(h_sib.at[layer], h_cat.at[sib_rows], l_h2)

    def gb_push(layer):
        return send(gb_cat.at[own_rows], gb_sib.at[layer], s_gb, r_gb, sibling)

    def gb_load2(layer):
        return pltpu.make_async_copy(gb_sib.at[layer], gb_cat.at[sib_rows], l_gb2)

    def dx_store():
        return pltpu.make_async_copy(gb_cat.at[own_rows], dx, l_dx)

    barrier = pltpu.get_barrier_semaphore()
    for to in (peer(0), peer(1), peer(2), sibling):
        pl.semaphore_signal(barrier, inc=1, device_id=to, device_id_type=MESH)
    top = layers - 1
    gb_first = pltpu.make_async_copy(dy, gb_cat.at[own_rows], l_gb)
    gb_first.start()
    for i in range(nu):
        a_load(top, i).start()
    for load in loads(top, 0, 0):
        load.start()
    pl.semaphore_wait(barrier, 4)
    dy_push = send(dy, gb_cat.at[sib_rows], s_gb, l_gb2, sibling)
    dy_push.start()
    for i in range(nu):
        a_first(i).start()
    gb_first.wait()
    g[...] = gb_cat[own_rows].astype(F32)
    dy_push.wait_send()
    for i in range(nu):
        a_first(i).wait_send()

    def layer_step(li, carry):
        layer = layers - 1 - li
        base = li * 2 * nu
        gb_load2(layer).wait()

        def first(i, carry):
            t = base + i
            a_load(layer, i).wait()
            a_load2(layer, i).wait()
            part = mm(a_cat[:, cols(i)], gb_cat[...], 0, 0)
            unit[t % SLOTS] = part.reshape(8, rows // 8, width).astype(BF16)

            @pl.when(i < nu - 1)
            def _():
                for load in loads(layer, i + 1, (i + 1) % 2):
                    load.start()

            comm(t)
            push_unit(t)

            @pl.when(i == 0)
            def _():
                h_push(layer).start()
                h_load(layer).start()

            @pl.when(i == hn)
            def _():
                h_push(layer).wait()
                h_load2(layer).start()

            @pl.when(layer > 0)
            def _():
                @pl.when(i > 0)
                def _():
                    a_push(layer - 1, i - 1).wait_send()

                a_push(layer - 1, i).start()

            for load in loads(layer, i, i % 2):
                load.wait()
            d_act = mm(gb_cat[own_rows], w2c[i % 2], 1, 1)
            du = (d_act * gelu_slope(uc[i % 2].astype(F32))).astype(BF16)

            @pl.when(jnp.logical_and(i >= 2, i < hn + 2))
            def _():
                du_push(layer, i - 2).wait_send()

            @pl.when(i < hn)
            def _():
                du_st[i % 2] = du

            @pl.when(i >= hn)
            def _():
                du_cat[own_rows, du_cols(i)] = du
                du_push(layer, i - hn).wait_recv()
                du_load(layer, i - hn).start()

            g[...] += mm(du, w1c[i % 2], 1, 1)

            @pl.when(i < hn)
            def _():
                du_push(layer, i).start()

            return carry

        lax.fori_loop(0, nu, first, 0)
        gb_cat[own_rows] = g[...].astype(BF16)
        h_load(layer).wait()
        h_load2(layer).wait()
        for i in range(hn):
            du_load(layer, i).wait()

        def second(i, carry):
            t = base + nu + i
            mi, fi = i % nm, i // nm
            part = mm(h_cat[:, cols(mi)], du_cat[:, pl.ds(pl.multiple_of(fi * width, 128), width)], 0, 0)
            unit[t % SLOTS] = part.reshape(8, rows // 8, width).astype(BF16)
            comm(t)
            push_unit(t)

            @pl.when(layer > 0)
            def _():
                @pl.when(i == 0)
                def _():
                    for load in loads(layer - 1, 0, 0):
                        load.start()
                    a_push(layer - 1, nu - 1).wait_send()
                    gb_push(layer - 1).start()

                @pl.when(i == hn)
                def _():
                    gb_push(layer - 1).wait()
                    gb_load2(layer - 1).start()

                a_push(layer - 1, i).wait_recv()
                a_load(layer - 1, i).start()
                a_load2(layer - 1, i).start()

            @pl.when(jnp.logical_and(layer == 0, i == 0))
            def _():
                dx_store().start()

            return carry

        lax.fori_loop(0, nu, second, 0)
        return carry

    lax.fori_loop(0, layers, layer_step, 0)

    def drain(t, carry):
        comm(t)
        return carry

    lax.fori_loop(units, units + 7 * LAG, drain, 0)
    dx_store().wait()


def backward(w_one, w_two, u, a, h, dy, rows):
    layers, width, wide = w_one.shape
    tokens = dy.shape[0]
    half = wide // 2
    nu = half // rows
    hn = nu // 2
    chunk = wide // nu
    units = 2 * nu * layers
    dma, reg = pltpu.SemaphoreType.DMA, pltpu.SemaphoreType.REGULAR
    hbm = pl.BlockSpec(memory_space=pl.ANY)
    sub = rows // 8
    shape = jax.ShapeDtypeStruct
    outs = [
        shape((units, 2, 8, sub, width), BF16),
        shape((tokens, width), BF16),
        shape((layers, tokens, half), BF16),
        shape((layers, tokens, width), BF16),
        shape((layers, tokens, half), BF16),
        shape((layers, tokens, width), BF16),
    ]
    scratch = [
        pltpu.VMEM((2 * tokens, half), BF16),
        pltpu.VMEM((2 * tokens, half), BF16),
        pltpu.VMEM((2 * tokens, width), BF16),
        pltpu.VMEM((2 * tokens, width), BF16),
        pltpu.VMEM((tokens, width), F32),
        pltpu.VMEM((2, chunk, width), BF16),
        pltpu.VMEM((2, width, chunk), BF16),
        pltpu.VMEM((2, tokens, chunk), BF16),
        pltpu.VMEM((2, tokens, chunk), BF16),
        pltpu.VMEM((SLOTS, 8, sub, width), BF16),
        pltpu.VMEM((RECV, 4, sub, width), BF16),
        pltpu.VMEM((RECV, 2, sub, width), BF16),
        pltpu.VMEM((RECV, 1, sub, width), BF16),
        *[dma((SLOTS,))] * 8,
        *[dma((RECV,))] * 3,
        *[dma((SLOTS,))] * 4,
        *[reg((RECV,))] * 3,
        dma((nu,)), dma((2, nu)), dma((nu,)), dma((nu,)),
        dma((hn,)), dma((hn,)), dma((hn,)),
        dma, dma, dma, dma,
        dma, dma, dma, dma,
        dma((2,)), dma((2,)), dma((2,)), dma,
    ]
    return pl.pallas_call(
        functools.partial(backward_body, layers=layers, tokens=tokens, width=width, wide=wide, rows=rows),
        out_shape=outs,
        in_specs=[hbm] * 6,
        out_specs=[hbm] * 6,
        scratch_shapes=scratch,
        compiler_params=pltpu.CompilerParams(collective_id=0, has_side_effects=True, vmem_limit_bytes=VMEM_LIMIT),
        name="backward",
    )(w_one, w_two, u, a, h, dy)


def assemble_body(tot_ref, out_ref):
    out_ref[0] = tot_ref[0, 0].reshape(out_ref.shape[1:])


def assemble(tot, layers, width, wide, rows):
    nu = wide // 2 // rows
    nm = width // rows
    nf = wide // width
    sub = rows // 8

    def call(grid, index, shape, out_index):
        return pl.pallas_call(
            assemble_body,
            grid=grid,
            out_shape=jax.ShapeDtypeStruct(shape, BF16),
            in_specs=[pl.BlockSpec((1, 1, 8, sub, width), index)],
            out_specs=pl.BlockSpec((1, rows, width), out_index),
            name="assemble",
        )(tot)

    one = call(
        (layers, nm, nf),
        lambda l, m, f: ((layers - 1 - l) * 2 * nu + nu + (f % (nf // 2)) * nm + m, f // (nf // 2), 0, 0, 0),
        (layers, width, wide),
        lambda l, m, f: (l, m, f),
    )
    two = call(
        (layers, 2 * nu),
        lambda l, j: ((layers - 1 - l) * 2 * nu + j % nu, j // nu, 0, 0, 0),
        (layers, wide, width),
        lambda l, j: (l, j, 0),
    )
    return one, two


def solution(mesh, rows=UNIT_ROWS):
    batch_spec = P(AXES)

    def per_device(w_one, w_two, x_loc, dy_loc):
        layers, width, wide = w_one.shape
        x = x_loc.reshape(-1, width)
        dy = dy_loc.reshape(-1, width)
        u, a, h = forward(x, w_one, w_two)
        tot, dx = backward(w_one, w_two, u, a, h, dy, rows)[:2]
        one, two = assemble(tot, layers, width, wide, rows)
        return one, two, dx.reshape(x_loc.shape)

    return jax.shard_map(per_device, mesh=mesh, in_specs=(P(), P(), batch_spec, batch_spec), out_specs=(P(), P(), batch_spec), check_vma=False)
```

time: 1880 us -> 921 us (0.49)
  waiting for transfers between devices: 1280 us -> 0 us
  Pallas kernels: 101 us -> 913 us
  matrix products: 479 us -> 0 us
    reduce_scatter x8 -> x0, waiting for transfers between devices: 853 us -> none  [total(): lax.psum_scatter(grad.astype(jnp.bfloat16), AXES, scatter_dimension=0, ti...]
    pallas_call x8 -> x4, Pallas kernels: 101 us -> 913 us  [the longest x1 695 us: backward(): pl.pallas_call(functools.partial(backward_body, layers=layers, tokens=tok...]
    dot_general x23 -> x0, matrix products: 479 us -> none  [dot(): lax.dot_general(lhs, rhs, (((lhs_dim,), (rhs_dim,)), ((), ())), preferred...]
    all_gather x8 -> x0, waiting for transfers between devices: 422 us -> none  [total(): return lax.all_gather(shard, AXES, axis=0, tiled=True)]
  transfers between devices with their start and end apart: 16 -> 0, of which waited for: 15 -> 0; matrix products, arithmetic and copies ran while one was open for 15% -> 0% of each run, Pallas kernels for 5% -> 0%
where the time goes in v2:
time: 921 us; the launch traced here: 914 us
  Pallas kernels  913 us (99%)
    pallas_call x1, Pallas kernels, backward(): pl.pallas_call(functools.partial(backward_body, layers=layers, tokens=tok...  695 us
    pallas_call x2, Pallas kernels, call(): pl.pallas_call(assemble_body, grid=grid, out_shape=jax.ShapeDtypeStruct(s...  118 us
    pallas_call x1, Pallas kernels, forward(): pl.pallas_call(functools.partial(forward_body, layers=layers, chunks=chun...  99.5 us

profile of v2, /device:TPU:0, one launch (start us, length us, event | category | flops | bytes accessed | tf_op | source)
XLA Modules:
  0.0 914.4 jit_solution(1404123056440017998)
XLA Ops:
  0.6 99.5 %forward.1 = (bf16[4,768,5120]{2,1,0:T(8,128)(2,1)}, bf16[4,768,5120]{2,1,0:T(8,128)(2,1)}, bf16[4,768,1280]{2,1,0:T(8,128)(2,1)}) custom-call(bf16[768,1280]{1,0:T(8,128)(2,1)} %bitcast.4, bf16[4,1280,5120]{2,1,0:T(8,128)(2,1)} %w1.1, bf16[4,5120,1280]{2,1,0:T(8,128)(2,1)} %w2.1), custom_call_target="tpu_custom_call" | custom-call | tf_op jit(solution)/shard_map/forward/pallas_call | solution.py:65
  100.1 694.8 %backward.1 = (bf16[80,2,8,32,1280]{4,3,2,1,0:T(8,128)(2,1)}, bf16[768,1280]{1,0:T(8,128)(2,1)}, bf16[4,768,2560]{2,1,0:T(8,128)(2,1)}, bf16[4,768,1280]{2,1,0:T...) custom-call(bf16[4,1280,5120]{2,1,0:T(8,128)(2,1)} %w1.1, bf16[4,5120,1280]{2,1,0:T(8,128)(2,1)} %w2.1, ...), custom_call_target="tpu_custom_call" | custom-call | tf_op jit(solution)/shard_map/backward/pallas_call | solution.py:490
  794.9 59.1 %assemble.3 = bf16[4,5120,1280]{2,1,0:T(8,128)(2,1)} custom-call(bf16[80,2,8,32,1280]{4,3,2,1,0:T(8,128)(2,1)} %get-tuple-element.11.tot_ref), custom_call_target="tpu_custom_call" | custom-call | tf_op jit(solution)/shard_map/assemble/pallas_call | solution.py:512
  854.0 0.0 copy-start
  854.0 59.2 %assemble.2 = bf16[4,1280,5120]{2,1,0:T(8,128)(2,1)} custom-call(bf16[80,2,8,32,1280]{4,3,2,1,0:T(8,128)(2,1)} %get-tuple-element.11.tot_ref), custom_call_target="tpu_custom_call" | custom-call | tf_op jit(solution)/shard_map/assemble/pallas_call | solution.py:512
  913.2 0.0 copy-done
  913.2 1.3 copy.8
Async XLA Ops:
  854.0 59.2 %copy-start = (bf16[768,1280]{1,0:T(8,128)(2,1)S(1)}, bf16[768,1280]{1,0:T(8,128)(2,1)}, u32[]{:S(2)}) copy-start(bf16[768,1280]{1,0:T(8,128)(2,1)} %get-tuple-element.12) | copy-start | bytes 5898244

commit v3 on v2

v3 whole, which is shorter than its diff:
```python
import functools

import jax
import jax.numpy as jnp
from jax import lax
from jax.experimental import pallas as pl
from jax.experimental.pallas import tpu as pltpu
from jax.sharding import PartitionSpec as P

AXES = ("replica", "data")
MESH = pl.DeviceIdType.MESH
BF16, F32 = jnp.bfloat16, jnp.float32
VMEM_LIMIT = 67_043_328
C0, C1 = 0.7978845608028654, 0.044715
UNIT_ROWS = 256
LAG = 3
SLOTS, RECV = 12, 8
X, Y, Z = 0, 1, 2


def gelu(v):
    return 0.5 * v * (1.0 + jnp.tanh(C0 * (v + C1 * (v * v * v))))


def gelu_slope(v):
    sq = v * v
    t = jnp.tanh(C0 * (v + C1 * (sq * v)))
    return 0.5 * (1.0 + t) + 0.5 * v * (1.0 - t * t) * (C0 * (1.0 + 3.0 * C1 * sq))


def mm(lhs, rhs, lhs_dim, rhs_dim):
    return lax.dot_general(lhs, rhs, (((lhs_dim,), (rhs_dim,)), ((), ())), preferred_element_type=F32)


def forward_body(z_ref, x_ref, w1_ref, w2_ref, u_ref, a_ref, h_ref, hid, acc, act_s, *, layers, chunks, rows):
    layer, j = pl.program_id(0), pl.program_id(1)
    part = rows // 2
    shift = z_ref[0] * part

    def pick(ref, k):
        return ref[:, pl.ds(pl.multiple_of(k * rows + shift, part), part)]

    @pl.when(jnp.logical_and(layer == 0, j == 0))
    def _():
        hid[...] = x_ref[...]

    @pl.when(j == 0)
    def _():
        for k in range(hid.shape[1] // rows):
            h_ref[0, :, k * part : (k + 1) * part] = pick(hid, k)
        acc[...] = hid[...].astype(F32)

    pre = mm(hid[...], w1_ref[0], 1, 0).astype(BF16)
    u_ref[0] = pre
    act = gelu(pre.astype(F32)).astype(BF16)
    act_s[...] = act

    @pl.when(layer < layers - 1)
    def _():
        acc[...] += mm(act, w2_ref[0], 1, 0)

        @pl.when(j == chunks - 1)
        def _():
            hid[...] = acc[...].astype(BF16)

    for k in range(act_s.shape[1] // rows):
        a_ref[0, :, k * part : (k + 1) * part] = pick(act_s, k)


def forward(z, x, w_one, w_two, rows):
    layers, width, wide = w_one.shape
    tokens = x.shape[0]
    chunk = width
    chunks = wide // chunk
    shape = jax.ShapeDtypeStruct
    return pl.pallas_call(
        functools.partial(forward_body, layers=layers, chunks=chunks, rows=rows),
        grid=(layers, chunks),
        out_shape=[shape((layers, tokens, wide), BF16), shape((layers, tokens, wide // 2), BF16), shape((layers, tokens, width // 2), BF16)],
        in_specs=[
            pl.BlockSpec(memory_space=pltpu.SMEM),
            pl.BlockSpec((tokens, width), lambda l, j: (0, 0)),
            pl.BlockSpec((1, width, chunk), lambda l, j: (l, 0, j)),
            pl.BlockSpec((1, chunk, width), lambda l, j: (l, j, 0)),
        ],
        out_specs=[
            pl.BlockSpec((1, tokens, chunk), lambda l, j: (l, 0, j)),
            pl.BlockSpec((1, tokens, chunk // 2), lambda l, j: (l, 0, j)),
            pl.BlockSpec((1, tokens, width // 2), lambda l, j: (l, 0, 0)),
        ],
        scratch_shapes=[pltpu.VMEM((tokens, width), BF16), pltpu.VMEM((tokens, width), F32), pltpu.VMEM((tokens, chunk), BF16)],
        compiler_params=pltpu.CompilerParams(vmem_limit_bytes=VMEM_LIMIT),
        cost_estimate=pl.CostEstimate(
            flops=(4 * layers - 2) * tokens * width * wide, bytes_accessed=4 * layers * width * wide, transcendentals=layers * tokens * wide
        ),
        name="forward",
    )(z, x, w_one, w_two)


def backward_body(
    w1, w2, u_own, u_nbr, a_own, a_nbr, h_own, h_nbr, dy_own, dy_nbr,
    tot, dx, a_sib, h_sib, du_sib, gb_sib,
    a_cat, du_cat, h_cat, gb_cat, g, w2c, w1c, uc, du_st, unit, rcv1, rcv2,
    s_rs1, s_rs2, s_ag1, s_ag2, s_ag3, s_fwd, s_own,
    r_rs1, r_rs2, r_ag1, r_ag2, r_ag3, r_fwd,
    c_rs1, c_rs2,
    s_a, r_a, l_a, l_a2, s_du, r_du, l_du, s_gb, r_gb, l_gb, l_gb2, s_h, r_h, l_h, l_h2, l_w2, l_w1, l_u, l_dx,
    *, layers, tokens, width, wide, rows,
):
    half = wide // 2
    part = rows // 2
    nu = half // rows
    nm = width // rows
    hn = nu // 2
    chunk = wide // nu
    units = 2 * nu * layers
    step = tokens // 2
    z, rest = lax.axis_index("replica"), lax.axis_index("data")
    core, x, y = rest % 2, (rest // 2) % 2, rest // 4

    def choose(axis):
        return (1 - axis) * (2 - axis) // 2, axis * (2 - axis), axis * (axis - 1) // 2

    def peer(axis):
        ex, ey, ez = choose(axis)
        px, py, pz = x + ex * (1 - 2 * x), y + ey * (1 - 2 * y), z + ez * (1 - 2 * z)
        return (pz, (py * 2 + px) * 2 + core)

    sibling = (z, (y * 2 + x) * 2 + 1 - core)

    def send(src, dst, ssem, rsem, to):
        return pltpu.make_async_remote_copy(src_ref=src, dst_ref=dst, send_sem=ssem, recv_sem=rsem, device_id=to, device_id_type=MESH)

    def place(n):
        mid = (n % 3) // 2
        a_axis = (1 - mid) * (n % 3) + mid * ((n // 3) % 2)
        b_axis = 1 - a_axis
        bit_a = x + a_axis * (y - x)
        bit_b = x + b_axis * (y - x)
        own = (1 - mid) * (4 * z + 2 * bit_a + bit_b) + mid * (4 * bit_a + 2 * z + bit_b)
        return mid, a_axis, b_axis, bit_a, bit_b, own

    def rs1(n):
        mid, a_axis, b_axis, bit_a, bit_b, own = place(n)
        return send(unit.at[n % SLOTS, pl.ds(2 - 2 * bit_a, 2)], rcv1.at[n % RECV], s_rs1.at[n % SLOTS], r_rs1.at[n % RECV], peer(a_axis))

    def rs2(n):
        mid, a_axis, b_axis, bit_a, bit_b, own = place(n)
        return send(unit.at[n % SLOTS, pl.ds(2 * bit_a + 1 - bit_b, 1)], rcv2.at[n % RECV], s_rs2.at[n % SLOTS], r_rs2.at[n % RECV], peer(b_axis))

    def own_copy(n):
        mid, a_axis, b_axis, bit_a, bit_b, own = place(n)
        return pltpu.make_async_copy(unit.at[n % SLOTS, pl.ds(2 * bit_a + bit_b, 1)], tot.at[n, core, pl.ds(own, 1)], s_own.at[n % SLOTS])

    def ag1(n):
        mid, a_axis, b_axis, bit_a, bit_b, own = place(n)
        return send(
            unit.at[n % SLOTS, pl.ds(2 * bit_a + bit_b, 1)], tot.at[n, core, pl.ds(own, 1)], s_ag1.at[n % SLOTS], r_ag1.at[n % SLOTS], peer(b_axis)
        )

    def ag2(n):
        mid, a_axis, b_axis, bit_a, bit_b, own = place(n)
        piece = tot.at[n, core, pl.ds(own // 2 * 2, 2)]
        return send(piece, piece, s_ag2.at[n % SLOTS], r_ag2.at[n % SLOTS], peer(a_axis + mid * (Z - a_axis)))

    def ag3(n):
        mid, a_axis, b_axis, bit_a, bit_b, own = place(n)
        piece = tot.at[n, core, pl.ds(own // 4 * 4, 4)]
        return send(piece, piece, s_ag3.at[n % SLOTS], r_ag3.at[n % SLOTS], peer(Z + mid * (a_axis - Z)))

    def fwd(n):
        piece = tot.at[n, core]
        return send(piece, piece, s_fwd.at[n % SLOTS], r_fwd.at[n % SLOTS], sibling)

    def add(n, block, rcv, j):
        slot = n % SLOTS
        unit[slot, block] = (unit[slot, block].astype(F32) + rcv[n % RECV, j].astype(F32)).astype(BF16)

    def credit(sem, n, axis):
        @pl.when(n + RECV < units)
        def _():
            pl.semaphore_signal(sem.at[n % RECV], inc=1, device_id=peer(axis), device_id_type=MESH)

    def spend(sem, n):
        @pl.when(n >= RECV)
        def _():
            pl.semaphore_wait(sem.at[n % RECV], 1)

    def live(n):
        return jnp.logical_and(n >= 0, n < units)

    def comm(t):
        n1, n2, n3, n4, n5, n6 = (t - k * LAG for k in range(1, 7))

        @pl.when(live(n2))
        def _():
            mid, a_axis, b_axis, bit_a, bit_b, own = place(n2)
            rs2(n2).wait_recv()
            add(n2, 2 * bit_a + bit_b, rcv2, 0)
            credit(c_rs2, n2, b_axis)
            rs1(n2).wait_send()

        @pl.when(live(n1))
        def _():
            mid, a_axis, b_axis, bit_a, bit_b, own = place(n1)
            rs1(n1).wait_recv()
            add(n1, 2 * bit_a + 1 - bit_b, rcv1, 1 - bit_b)
            add(n1, 2 * bit_a + bit_b, rcv1, bit_b)
            credit(c_rs1, n1, a_axis)

        @pl.when(live(n2))
        def _():
            own_copy(n2).start()
            ag1(n2).start()

        @pl.when(live(n1))
        def _():
            spend(c_rs2, n1)
            rs2(n1).start()

        @pl.when(live(n3))
        def _():
            rs2(n3).wait_send()
            own_copy(n3).wait()
            ag1(n3).wait()
            ag2(n3).start()

        @pl.when(live(n4))
        def _():
            ag2(n4).wait()
            ag3(n4).start()

        @pl.when(live(n5))
        def _():
            ag3(n5).wait()
            fwd(n5).start()

        @pl.when(live(n6))
        def _():
            fwd(n6).wait()

    def push_unit(t):
        spend(c_rs1, t)
        rs1(t).start()

    sets = (0, 1)
    us, as_, hs, dys = (u_own, u_nbr), (a_own, a_nbr), (h_own, h_nbr), (dy_own, dy_nbr)

    def mine(k):
        return pl.ds(k * tokens, tokens)

    def theirs(k):
        return pl.ds((2 + k) * tokens, tokens)

    def chunk_at(i):
        late = i // hn
        return pl.multiple_of(((1 - core) + late * (2 * core - 1)) * half + (i % hn) * chunk, 128)

    def loads(layer, i):
        f0, slot = chunk_at(i), i % 2
        return (
            pltpu.make_async_copy(w2.at[layer, pl.ds(f0, chunk)], w2c.at[slot], l_w2.at[slot]),
            pltpu.make_async_copy(w1.at[layer, :, pl.ds(f0, chunk)], w1c.at[slot], l_w1.at[slot]),
            *(pltpu.make_async_copy(us[k].at[layer, :, pl.ds(f0, chunk)], uc.at[slot, k], l_u.at[slot, k]) for k in sets),
        )

    def cols(i, size):
        return pl.ds(pl.multiple_of(i * size, 128), size)

    def a_load(layer, k):
        return pltpu.make_async_copy(as_[k].at[layer, :, cols(core, half // 2)], a_cat.at[mine(k)], l_a.at[k])

    def a_load2(layer, k):
        return pltpu.make_async_copy(a_sib.at[layer, k], a_cat.at[theirs(k)], l_a2.at[k])

    def a_first(k):
        return send(as_[k].at[layers - 1, :, cols(1 - core, half // 2)], a_cat.at[theirs(k)], s_a.at[k], l_a2.at[k], sibling)

    def a_push(layer, k):
        return send(as_[k].at[layer, :, cols(1 - core, half // 2)], a_sib.at[layer, k], s_a.at[k], r_a.at[k], sibling)

    def du_push(layer, i, k):
        return send(du_st.at[k], du_sib.at[layer, k, :, cols(i % hn, chunk)], s_du.at[k], r_du.at[i % hn, k], sibling)

    def du_load(layer, i, k):
        return pltpu.make_async_copy(du_sib.at[layer, k, :, cols(i % hn, chunk)], du_cat.at[theirs(k), cols(i % hn, chunk)], l_du.at[i % hn, k])

    def h_push(layer, k):
        return send(hs[k].at[layer], h_sib.at[layer, k], s_h.at[k], r_h.at[k], sibling)

    def h_load(layer, k):
        return pltpu.make_async_copy(hs[k].at[layer], h_cat.at[mine(k)], l_h.at[k])

    def h_load2(layer, k):
        return pltpu.make_async_copy(h_sib.at[layer, k], h_cat.at[theirs(k)], l_h2.at[k])

    def gb_push(layer, k):
        return send(gb_cat.at[mine(k)], gb_sib.at[layer, k], s_gb.at[k], r_gb.at[k], sibling)

    def gb_load2(layer, k):
        return pltpu.make_async_copy(gb_sib.at[layer, k], gb_cat.at[theirs(k)], l_gb2.at[k])

    def gb_first(k):
        return pltpu.make_async_copy(dys[k], gb_cat.at[mine(k)], l_gb.at[k])

    def dy_push(k):
        return send(dys[k], gb_cat.at[theirs(k)], s_gb.at[k], l_gb2.at[k], sibling)

    def dx_store():
        return pltpu.make_async_copy(gb_cat.at[mine(0)], dx, l_dx)

    barrier = pltpu.get_barrier_semaphore()
    for to in (peer(X), peer(Y), peer(Z), sibling):
        pl.semaphore_signal(barrier, inc=1, device_id=to, device_id_type=MESH)
    top = layers - 1
    for k in sets:
        gb_first(k).start()
        a_load(top, k).start()
    for load in loads(top, 0):
        load.start()
    pl.semaphore_wait(barrier, 4)
    for k in sets:
        dy_push(k).start()
        a_first(k).start()
    for k in sets:
        gb_first(k).wait()
        g[mine(k)] = gb_cat[mine(k)].astype(F32)
    for k in sets:
        dy_push(k).wait_send()
        a_first(k).wait_send()

    def layer_step(li, carry):
        layer = layers - 1 - li
        base = li * 2 * nu
        for k in sets:
            gb_load2(layer, k).wait()
            a_load(layer, k).wait()
            a_load2(layer, k).wait()

        def first(i, carry):
            t = base + i
            out = mm(a_cat[:, cols(i, part)], gb_cat[...], 0, 0)
            unit[t % SLOTS] = out.reshape(4, rows // 8, width).astype(BF16)

            @pl.when(i < nu - 1)
            def _():
                for load in loads(layer, i + 1):
                    load.start()

            comm(t)
            push_unit(t)

            @pl.when(i == 0)
            def _():
                for k in sets:
                    h_push(layer, k).start()
                    h_load(layer, k).start()

            @pl.when(i == hn)
            def _():
                for k in sets:
                    h_push(layer, k).wait()
                    h_load2(layer, k).start()

            @pl.when(jnp.logical_and(layer > 0, i == 2))
            def _():
                for k in sets:
                    a_push(layer - 1, k).start()

            for load in loads(layer, i):
                load.wait()

            def token_set(k, carry):
                @pl.when(jnp.logical_and(i >= 1, i <= hn))
                def _():
                    du_push(layer, i - 1, k).wait_send()

                def block(b, carry):
                    at = pl.ds(pl.multiple_of(b * step, 16), step)
                    rows_b = pl.ds(pl.multiple_of(k * tokens + b * step, 16), step)
                    d_act = mm(gb_cat[rows_b], w2c[i % 2], 1, 1)
                    du = (d_act * gelu_slope(uc[i % 2, k, at].astype(F32))).astype(BF16)

                    @pl.when(i < hn)
                    def _():
                        du_st[k, at] = du

                    @pl.when(i >= hn)
                    def _():
                        du_cat[rows_b, cols(i % hn, chunk)] = du

                    @pl.when(jnp.logical_or(layer > 0, k == 0))
                    def _():
                        g[rows_b] += mm(du, w1c[i % 2], 1, 1)

                    return carry

                lax.fori_loop(0, tokens // step, block, 0)

                @pl.when(i < hn)
                def _():
                    du_push(layer, i, k).start()

                @pl.when(i >= hn)
                def _():
                    du_push(layer, i - hn, k).wait_recv()
                    du_load(layer, i - hn, k).start()

                return carry

            lax.fori_loop(0, 2, token_set, 0)
            return carry

        lax.fori_loop(0, nu, first, 0)
        for k in sets:
            gb_cat[mine(k)] = g[mine(k)].astype(BF16)
        for k in sets:
            h_load(layer, k).wait()
            h_load2(layer, k).wait()
            for i in range(hn):
                du_load(layer, i, k).wait()

        def second(i, carry):
            t = base + nu + i
            mi, fi = i % nm, i // nm
            out = mm(h_cat[:, cols(mi, part)], du_cat[:, cols(fi, width)], 0, 0)
            unit[t % SLOTS] = out.reshape(4, rows // 8, width).astype(BF16)
            comm(t)
            push_unit(t)

            @pl.when(layer > 0)
            def _():
                @pl.when(i == 0)
                def _():
                    for load in loads(layer - 1, 0):
                        load.start()
                    for k in sets:
                        a_push(layer - 1, k).wait()
                        a_load(layer - 1, k).start()
                        a_load2(layer - 1, k).start()
                    for k in sets:
                        gb_push(layer - 1, k).start()

                @pl.when(i == hn)
                def _():
                    for k in sets:
                        gb_push(layer - 1, k).wait()
                        gb_load2(layer - 1, k).start()

            @pl.when(jnp.logical_and(layer == 0, i == 0))
            def _():
                dx_store().start()

            return carry

        lax.fori_loop(0, nu, second, 0)
        return carry

    lax.fori_loop(0, layers, layer_step, 0)

    def drain(t, carry):
        comm(t)
        return carry

    lax.fori_loop(units, units + 6 * LAG, drain, 0)
    dx_store().wait()


def backward(w_one, w_two, us, as_, hs, dys, rows):
    layers, width, wide = w_one.shape
    tokens = dys[0].shape[0]
    half = wide // 2
    nu = half // rows
    hn = nu // 2
    chunk = wide // nu
    units = 2 * nu * layers
    dma, reg = pltpu.SemaphoreType.DMA, pltpu.SemaphoreType.REGULAR
    hbm = pl.BlockSpec(memory_space=pl.ANY)
    sub = rows // 8
    shape = jax.ShapeDtypeStruct
    outs = [
        shape((units, 2, 8, sub, width), BF16),
        shape((tokens, width), BF16),
        shape((layers, 2, tokens, half // 2), BF16),
        shape((layers, 2, tokens, width // 2), BF16),
        shape((layers, 2, tokens, half), BF16),
        shape((layers, 2, tokens, width), BF16),
    ]
    scratch = [
        pltpu.VMEM((4 * tokens, half // 2), BF16),
        pltpu.VMEM((4 * tokens, half), BF16),
        pltpu.VMEM((4 * tokens, width // 2), BF16),
        pltpu.VMEM((4 * tokens, width), BF16),
        pltpu.VMEM((2 * tokens, width), F32),
        pltpu.VMEM((2, chunk, width), BF16),
        pltpu.VMEM((2, width, chunk), BF16),
        pltpu.VMEM((2, 2, tokens, chunk), BF16),
        pltpu.VMEM((2, tokens, chunk), BF16),
        pltpu.VMEM((SLOTS, 4, sub, width), BF16),
        pltpu.VMEM((RECV, 2, sub, width), BF16),
        pltpu.VMEM((RECV, 1, sub, width), BF16),
        *[dma((SLOTS,))] * 7,
        *[dma((RECV,))] * 2,
        *[dma((SLOTS,))] * 4,
        *[reg((RECV,))] * 2,
        *[dma((2,))] * 4,
        dma((2,)), dma((hn, 2)), dma((hn, 2)),
        *[dma((2,))] * 8,
        dma((2,)), dma((2,)), dma((2, 2)), dma,
    ]
    return pl.pallas_call(
        functools.partial(backward_body, layers=layers, tokens=tokens, width=width, wide=wide, rows=rows),
        out_shape=outs,
        in_specs=[hbm] * 10,
        out_specs=[hbm] * 6,
        scratch_shapes=scratch,
        compiler_params=pltpu.CompilerParams(collective_id=0, has_side_effects=True, vmem_limit_bytes=VMEM_LIMIT),
        name="backward",
    )(w_one, w_two, *us, *as_, *hs, *dys)


COPY_SLOTS, COPY_LEAD = 24, 10


def assemble_body(tot, one, two, buf, s_in, s_out, *, layers, nu, nm, width):
    items = 4 * nu * layers

    def load(j):
        return pltpu.make_async_copy(tot.at[j // 2, j % 2], buf.at[j % COPY_SLOTS], s_in.at[j % COPY_SLOTS])

    def stores(j, run):
        n, core = j // 2, j % 2
        layer, i, slot = layers - 1 - n // (2 * nu), n % nu, j % COPY_SLOTS
        mid = (n % 3) // 2
        for q in range(4):
            src = (1 - mid) * q + mid * (q % 2 * 2 + q // 2)
            piece = buf.at[slot, pl.ds(src * 2, 2)]

            @pl.when((n // nu) % 2 == 0)
            def _():
                run(pltpu.make_async_copy(piece, two.at[layer, core * nu + i, pl.ds(2 * q, 2)], s_out.at[slot, q]))

            @pl.when((n // nu) % 2 == 1)
            def _():
                cols = pl.ds(pl.multiple_of((core * (nu // nm) + i // nm) * width, 128), width)
                run(pltpu.make_async_copy(piece, one.at[layer, i % nm, pl.ds(2 * q, 2), :, cols], s_out.at[slot, q]))

    def step(j, carry):
        @pl.when(j >= COPY_SLOTS)
        def _():
            stores(j - COPY_SLOTS, lambda c: c.wait())

        @pl.when(j < items)
        def _():
            load(j).start()

        @pl.when(jnp.logical_and(j >= COPY_LEAD, j < items + COPY_LEAD))
        def _():
            load(j - COPY_LEAD).wait()
            stores(j - COPY_LEAD, lambda c: c.start())

        return carry

    lax.fori_loop(0, items + COPY_SLOTS, step, 0)


def assemble(tot, layers, width, wide, rows):
    nu, nm, sub = wide // 2 // rows, width // rows, rows // 8
    shape = jax.ShapeDtypeStruct
    hbm = pl.BlockSpec(memory_space=pl.ANY)
    one, two = pl.pallas_call(
        functools.partial(assemble_body, layers=layers, nu=nu, nm=nm, width=width),
        out_shape=[shape((layers, nm, 8, sub, wide), BF16), shape((layers, 2 * nu, 8, sub, width), BF16)],
        in_specs=[hbm],
        out_specs=[hbm, hbm],
        scratch_shapes=[pltpu.VMEM((COPY_SLOTS, 8, sub, width), BF16), pltpu.SemaphoreType.DMA((COPY_SLOTS,)), pltpu.SemaphoreType.DMA((COPY_SLOTS, 4))],
        compiler_params=pltpu.CompilerParams(vmem_limit_bytes=VMEM_LIMIT),
        name="assemble",
    )(tot)
    return one.reshape(layers, width, wide), two.reshape(layers, wide, width)


def solution(mesh, rows=UNIT_ROWS):
    batch_spec = P(AXES)

    def per_device(w_one, w_two, x_loc, dy_loc):
        layers, width, wide = w_one.shape
        x = x_loc.reshape(-1, width)
        dy = dy_loc.reshape(-1, width)
        swap = [(0, 1), (1, 0)]
        x_nbr = lax.ppermute(x, "replica", swap)
        dy_nbr = lax.ppermute(dy, "replica", swap)
        z = jnp.full((1,), lax.axis_index("replica"), jnp.int32)
        kept = [forward(z, tokens, w_one, w_two, rows) for tokens in (x, x_nbr)]
        us, as_, hs = zip(*kept)
        tot, dx = backward(w_one, w_two, us, as_, hs, (dy, dy_nbr), rows)[:2]
        one, two = assemble(tot, layers, width, wide, rows)
        return one, two, dx.reshape(x_loc.shape)

    return jax.shard_map(per_device, mesh=mesh, in_specs=(P(), P(), batch_spec, batch_spec), out_specs=(P(), P(), batch_spec), check_vma=False)
```

time: 921 us -> 921 us (level)
    pallas_call x1 -> x2, Pallas kernels: 99.5 us -> 200 us  [forward(): pl.pallas_call(functools.partial(forward_body, layers=layers, chunks=chun...]
    pallas_call x2 -> x1, Pallas kernels: 118 us -> 67 us  [assemble(): pl.pallas_call(functools.partial(assemble_body, layers=layers, nu=nu, nm=...]
    pallas_call x1, Pallas kernels: 695 us -> 647 us  [backward(): pl.pallas_call(functools.partial(backward_body, layers=layers, tokens=tok...]
  transfers between devices with their start and end apart: 0 -> 2, of which waited for: 0 -> 0; matrix products, arithmetic and copies ran while one was open for 0% -> 0% of each run, Pallas kernels for 0% -> 22%
where the time goes in v3:
time: 921 us
  Pallas kernels  914 us (99%)
    pallas_call x1, Pallas kernels, backward(): pl.pallas_call(functools.partial(backward_body, layers=layers, tokens=tok...  647 us
    pallas_call x2, Pallas kernels, forward(): pl.pallas_call(functools.partial(forward_body, layers=layers, chunks=chun...  200 us
    pallas_call x1, Pallas kernels, assemble(): pl.pallas_call(functools.partial(assemble_body, layers=layers, nu=nu, nm=...  67 us
  transfers between devices with their start and end apart: 2, of which 0 were waited for; matrix products, arithmetic and copies ran while one was open for 0% of the time, Pallas kernels for 22%

profile of v3, /device:TPU:0, one launch (start us, length us, event | category | flops | bytes accessed | tf_op | source)
XLA Modules:
  0.0 920.7 jit_solution(9188693215881943709)
XLA Ops:
  0.6 3.3 collective-permute-start
  4.0 0.1 collective-permute-start.1
  4.0 99.8 %forward.2 = (bf16[4,768,5120]{2,1,0:T(8,128)(2,1)}, bf16[4,768,2560]{2,1,0:T(8,128)(2,1)}, bf16[4,768,640]{2,1,0:T(8,128)(2,1)}) custom-call(s32[1]{0:T(128)} %bitcast.z_ref, bf16[768,1280]{1,0:T(8,128)(2,1)} %bitcast.12, bf16[4,1280,5120]{2,1,0:T(8,128)(2,1)} %w1.1, bf16[4,5120,1280]{2,1,0:T(8,128)(2,1)} %w2.1), custom_call_target="tpu_custom_call" | custom-call | flops 70464307200 | bytes 104857600 | tf_op jit(solution)/shard_map/forward/pallas_call | solution.py:76
  103.9 0.0 collective-permute-done.x_ref
  103.9 99.9 %forward.3 = (bf16[4,768,5120]{2,1,0:T(8,128)(2,1)}, bf16[4,768,2560]{2,1,0:T(8,128)(2,1)}, bf16[4,768,640]{2,1,0:T(8,128)(2,1)}) custom-call(s32[1]{0:T(128)} %bitcast.z_ref, bf16[768,1280]{1,0:T(8,128)(2,1)} %collective-permute-done.x_ref, bf16[4,1280,5120]{2,1,0:T(8,128)(2,1)} %w1.1, bf16[4,5120,1280]{2,1,0:T(8,128)(2,1)} %w2.1), custom_call_target="tpu_custom_call" | custom-call | flops 70464307200 | bytes 104857600 | tf_op jit(solution)/shard_map/forward/pallas_call | solution.py:76
  203.7 0.0 collective-permute-done.1.dy_nbr
  203.7 647.0 %backward.1 = (bf16[80,2,8,32,1280]{4,3,2,1,0:T(8,128)(2,1)}, bf16[768,1280]{1,0:T(8,128)(2,1)}, bf16[4,2,768,1280]{3,2,1,0:T(8,128)(2,1)}, bf16[4,2,768,640]{3,...) custom-call(bf16[4,1280,5120]{2,1,0:T(8,128)(2,1)} %w1.1, ...), custom_call_target="tpu_custom_call" | custom-call | tf_op jit(solution)/shard_map/backward/pallas_call | solution.py:511
  850.7 67.0 %assemble.1 = (bf16[4,5,8,32,5120]{4,3,2,1,0:T(8,128)(2,1)}, bf16[4,20,8,32,1280]{4,3,2,1,0:T(8,128)(2,1)}) custom-call(bf16[80,2,8,32,1280]{4,3,2,1,0:T(8,128)(2,1)} %get-tuple-element.19.tot), custom_call_target="tpu_custom_call" | custom-call | tf_op jit(solution)/shard_map/assemble/pallas_call | solution.py:571
  917.7 2.9 copy.8
Async XLA Ops:
  0.6 103.2 %collective-permute-start = (bf16[768,1280]{1,0:T(8,128)(2,1)}, bf16[768,1280]{1,0:T(8,128)(2,1)}, u32[]{:S(2)}, u32[]{:S(2)}) collective-permute-start(bf16[768,1280]{1,0:T(8,128)(2,1)} %bitcast.11), channel_id=1, source_target_pairs={{0,8},{8,0},{1,9},{9,1},{2,10},{10,2},{3,11},{11,3},{4,12},{12,4},... | collective-permute-start | bytes 5898248 | tf_op jit(solution)/shard_map/ppermute | solution.py:591
  4.0 199.7 %collective-permute-start.1 = (bf16[768,1280]{1,0:T(8,128)(2,1)}, bf16[768,1280]{1,0:T(8,128)(2,1)}, u32[]{:S(2)}, u32[]{:S(2)}) collective-permute-start(bf16[768,1280]{1,0:T(8,128)(2,1)} %bitcast.6), channel_id=1, source_target_pairs={{0,8},{8,0},{1,9},{9,1},{2,10},{10,2},{3,11},{11,3},{4,12},{12,4},... | collective-permute-start | bytes 5898248 | tf_op jit(solution)/shard_map/ppermute | solution.py:592

commit v4 on v3

--- a/solution.py
+++ b/solution.py
@@ -14,7 +14,7 @@
 C0, C1 = 0.7978845608028654, 0.044715
 UNIT_ROWS = 256
 LAG = 3
-SLOTS, RECV = 12, 8
+SLOTS, RECV, PARTS, RECV0 = 12, 8, 2, 4
 X, Y, Z = 0, 1, 2
 
 
@@ -99,19 +99,18 @@
 
 def backward_body(
     w1, w2, u_own, u_nbr, a_own, a_nbr, h_own, h_nbr, dy_own, dy_nbr,
-    tot, dx, a_sib, h_sib, du_sib, gb_sib,
-    a_cat, du_cat, h_cat, gb_cat, g, w2c, w1c, uc, du_st, unit, rcv1, rcv2,
-    s_rs1, s_rs2, s_ag1, s_ag2, s_ag3, s_fwd, s_own,
-    r_rs1, r_rs2, r_ag1, r_ag2, r_ag3, r_fwd,
-    c_rs1, c_rs2,
-    s_a, r_a, l_a, l_a2, s_du, r_du, l_du, s_gb, r_gb, l_gb, l_gb2, s_h, r_h, l_h, l_h2, l_w2, l_w1, l_u, l_dx,
+    tot, dx,
+    a_cat, du_cat, h_cat, gb_cat, g, w2c, w1c, uc, unit, part0, rcv0, rcv1, rcv2,
+    s_rs1, s_rs2, s_ag1, s_ag2, s_ag3, s_fwd, s_own, r_ag1, r_ag2, r_ag3, r_fwd,
+    r_rs1, r_rs2, c_rs1, c_rs2, s_rs0, r_rs0, c_rs0,
+    l_a, l_gb, l_h, l_w2, l_w1, l_u, l_dx,
     *, layers, tokens, width, wide, rows,
 ):
     half = wide // 2
     part = rows // 2
     nu = half // rows
     nm = width // rows
-    hn = nu // 2
+    nf = nu // nm
     chunk = wide // nu
     units = 2 * nu * layers
     step = tokens // 2
@@ -140,6 +139,9 @@
         own = (1 - mid) * (4 * z + 2 * bit_a + bit_b) + mid * (4 * bit_a + 2 * z + bit_b)
         return mid, a_axis, b_axis, bit_a, bit_b, own
 
+    def rs0(n):
+        return send(part0.at[n % PARTS], rcv0.at[n % RECV0], s_rs0.at[n % PARTS], r_rs0.at[n % RECV0], sibling)
+
     def rs1(n):
         mid, a_axis, b_axis, bit_a, bit_b, own = place(n)
         return send(unit.at[n % SLOTS, pl.ds(2 - 2 * bit_a, 2)], rcv1.at[n % RECV], s_rs1.at[n % SLOTS], r_rs1.at[n % RECV], peer(a_axis))
@@ -172,41 +174,50 @@
         piece = tot.at[n, core]
         return send(piece, piece, s_fwd.at[n % SLOTS], r_fwd.at[n % SLOTS], sibling)
 
-    def add(n, block, rcv, j):
-        slot = n % SLOTS
-        unit[slot, block] = (unit[slot, block].astype(F32) + rcv[n % RECV, j].astype(F32)).astype(BF16)
-
-    def credit(sem, n, axis):
-        @pl.when(n + RECV < units)
-        def _():
-            pl.semaphore_signal(sem.at[n % RECV], inc=1, device_id=peer(axis), device_id_type=MESH)
-
-    def spend(sem, n):
-        @pl.when(n >= RECV)
-        def _():
-            pl.semaphore_wait(sem.at[n % RECV], 1)
+    def add(n, block, rcv, slot, j):
+        unit[n % SLOTS, block] = (unit[n % SLOTS, block].astype(F32) + rcv[slot, j].astype(F32)).astype(BF16)
+
+    def credit(sem, n, slots, to):
+        @pl.when(n + slots < units)
+        def _():
+            pl.semaphore_signal(sem.at[n % slots], inc=1, device_id=to, device_id_type=MESH)
+
+    def spend(sem, n, slots):
+        @pl.when(n >= slots)
+        def _():
+            pl.semaphore_wait(sem.at[n % slots], 1)
 
     def live(n):
         return jnp.logical_and(n >= 0, n < units)
 
     def comm(t):
-        n1, n2, n3, n4, n5, n6 = (t - k * LAG for k in range(1, 7))
+        n0, n1, n2, n3, n4, n5 = (t - 1 - k * LAG for k in range(6))
+        n6 = n5 - 2
 
         @pl.when(live(n2))
         def _():
             mid, a_axis, b_axis, bit_a, bit_b, own = place(n2)
             rs2(n2).wait_recv()
-            add(n2, 2 * bit_a + bit_b, rcv2, 0)
-            credit(c_rs2, n2, b_axis)
+            add(n2, 2 * bit_a + bit_b, rcv2, n2 % RECV, 0)
+            credit(c_rs2, n2, RECV, peer(b_axis))
             rs1(n2).wait_send()
 
         @pl.when(live(n1))
         def _():
             mid, a_axis, b_axis, bit_a, bit_b, own = place(n1)
             rs1(n1).wait_recv()
-            add(n1, 2 * bit_a + 1 - bit_b, rcv1, 1 - bit_b)
-            add(n1, 2 * bit_a + bit_b, rcv1, bit_b)
-            credit(c_rs1, n1, a_axis)
+            add(n1, 2 * bit_a + 1 - bit_b, rcv1, n1 % RECV, 1 - bit_b)
+            add(n1, 2 * bit_a + bit_b, rcv1, n1 % RECV, bit_b)
+            credit(c_rs1, n1, RECV, peer(a_axis))
+
+        @pl.when(live(n0))
+        def _():
+            mid, a_axis, b_axis, bit_a, bit_b, own = place(n0)
+            rs0(n0).wait()
+            for first in (2 - 2 * bit_a, 2 * bit_a):
+                for j in range(2):
+                    add(n0, first + j, rcv0, n0 % RECV0, first + j)
+            credit(c_rs0, n0, RECV0, sibling)
 
         @pl.when(live(n2))
         def _():
@@ -215,8 +226,13 @@
 
         @pl.when(live(n1))
         def _():
-            spend(c_rs2, n1)
+            spend(c_rs2, n1, RECV)
             rs2(n1).start()
+
+        @pl.when(live(n0))
+        def _():
+            spend(c_rs1, n0, RECV)
+            rs1(n0).start()
 
         @pl.when(live(n3))
         def _():
@@ -240,24 +256,17 @@
             fwd(n6).wait()
 
     def push_unit(t):
-        spend(c_rs1, t)
-        rs1(t).start()
+        spend(c_rs0, t, RECV0)
+        rs0(t).start()
 
     sets = (0, 1)
     us, as_, hs, dys = (u_own, u_nbr), (a_own, a_nbr), (h_own, h_nbr), (dy_own, dy_nbr)
 
-    def mine(k):
+    def of(k):
         return pl.ds(k * tokens, tokens)
 
-    def theirs(k):
-        return pl.ds((2 + k) * tokens, tokens)
-
-    def chunk_at(i):
-        late = i // hn
-        return pl.multiple_of(((1 - core) + late * (2 * core - 1)) * half + (i % hn) * chunk, 128)
-
     def loads(layer, i):
-        f0, slot = chunk_at(i), i % 2
+        f0, slot = pl.multiple_of(i * chunk, 128), i % 2
         return (
             pltpu.make_async_copy(w2.at[layer, pl.ds(f0, chunk)], w2c.at[slot], l_w2.at[slot]),
             pltpu.make_async_copy(w1.at[layer, :, pl.ds(f0, chunk)], w1c.at[slot], l_w1.at[slot]),
@@ -268,79 +277,46 @@
         return pl.ds(pl.multiple_of(i * size, 128), size)
 
     def a_load(layer, k):
-        return pltpu.make_async_copy(as_[k].at[layer, :, cols(core, half // 2)], a_cat.at[mine(k)], l_a.at[k])
-
-    def a_load2(layer, k):
-        return pltpu.make_async_copy(a_sib.at[layer, k], a_cat.at[theirs(k)], l_a2.at[k])
-
-    def a_first(k):
-        return send(as_[k].at[layers - 1, :, cols(1 - core, half // 2)], a_cat.at[theirs(k)], s_a.at[k], l_a2.at[k], sibling)
-
-    def a_push(layer, k):
-        return send(as_[k].at[layer, :, cols(1 - core, half // 2)], a_sib.at[layer, k], s_a.at[k], r_a.at[k], sibling)
-
-    def du_push(layer, i, k):
-        return send(du_st.at[k], du_sib.at[layer, k, :, cols(i % hn, chunk)], s_du.at[k], r_du.at[i % hn, k], sibling)
-
-    def du_load(layer, i, k):
-        return pltpu.make_async_copy(du_sib.at[layer, k, :, cols(i % hn, chunk)], du_cat.at[theirs(k), cols(i % hn, chunk)], l_du.at[i % hn, k])
-
-    def h_push(layer, k):
-        return send(hs[k].at[layer], h_sib.at[layer, k], s_h.at[k], r_h.at[k], sibling)
+        return pltpu.make_async_copy(as_[k].at[layer], a_cat.at[of(k)], l_a.at[k])
 
     def h_load(layer, k):
-        return pltpu.make_async_copy(hs[k].at[layer], h_cat.at[mine(k)], l_h.at[k])
-
-    def h_load2(layer, k):
-        return pltpu.make_async_copy(h_sib.at[layer, k], h_cat.at[theirs(k)], l_h2.at[k])
-
-    def gb_push(layer, k):
-        return send(gb_cat.at[mine(k)], gb_sib.at[layer, k], s_gb.at[k], r_gb.at[k], sibling)
-
-    def gb_load2(layer, k):
-        return pltpu.make_async_copy(gb_sib.at[layer, k], gb_cat.at[theirs(k)], l_gb2.at[k])
-
-    def gb_first(k):
-        return pltpu.make_async_copy(dys[k], gb_cat.at[mine(k)], l_gb.at[k])
-
-    def dy_push(k):
-        return send(dys[k], gb_cat.at[theirs(k)], s_gb.at[k], l_gb2.at[k], sibling)
+        return pltpu.make_async_copy(hs[k].at[layer], h_cat.at[of(k)], l_h.at[k])
+
+    def gb_load(k):
+        return pltpu.make_async_copy(dys[k], gb_cat.at[of(k)], l_gb.at[k])
 
     def dx_store():
-        return pltpu.make_async_copy(gb_cat.at[mine(0)], dx, l_dx)
+        return pltpu.make_async_copy(gb_cat.at[of(0)], dx, l_dx)
+
+    def blocks(out):
+        return out.reshape(4, rows // 8, width).astype(BF16)
 
     barrier = pltpu.get_barrier_semaphore()
     for to in (peer(X), peer(Y), peer(Z), sibling):
         pl.semaphore_signal(barrier, inc=1, device_id=to, device_id_type=MESH)
-    top = layers - 1
     for k in sets:
-        gb_first(k).start()
-        a_load(top, k).start()
-    for load in loads(top, 0):
+        gb_load(k).start()
+        a_load(layers - 1, k).start()
+    for load in loads(layers - 1, 0):
         load.start()
+    for k in sets:
+        gb_load(k).wait()
+        g[of(k)] = gb_cat[of(k)].astype(F32)
     pl.semaphore_wait(barrier, 4)
-    for k in sets:
-        dy_push(k).start()
-        a_first(k).start()
-    for k in sets:
-        gb_first(k).wait()
-        g[mine(k)] = gb_cat[mine(k)].astype(F32)
-    for k in sets:
-        dy_push(k).wait_send()
-        a_first(k).wait_send()
 
     def layer_step(li, carry):
         layer = layers - 1 - li
         base = li * 2 * nu
         for k in sets:
-            gb_load2(layer, k).wait()
             a_load(layer, k).wait()
-            a_load2(layer, k).wait()
+            h_load(layer, k).start()
 
         def first(i, carry):
             t = base + i
-            out = mm(a_cat[:, cols(i, part)], gb_cat[...], 0, 0)
-            unit[t % SLOTS] = out.reshape(4, rows // 8, width).astype(BF16)
+            lhs = jnp.concatenate([a_cat[:, cols((1 - core) * nu + i, part)], a_cat[:, cols(core * nu + i, part)]], axis=1)
+            out = mm(lhs, gb_cat[...], 0, 0)
+            part0[t % PARTS] = blocks(out[:part])
+            unit[t % SLOTS] = blocks(out[part:])
 
             @pl.when(i < nu - 1)
             def _():
@@ -350,107 +326,51 @@
             comm(t)
             push_unit(t)
 
-            @pl.when(i == 0)
-            def _():
-                for k in sets:
-                    h_push(layer, k).start()
-                    h_load(layer, k).start()
-
-            @pl.when(i == hn)
-            def _():
-                for k in sets:
-                    h_push(layer, k).wait()
-                    h_load2(layer, k).start()
-
-            @pl.when(jnp.logical_and(layer > 0, i == 2))
-            def _():
-                for k in sets:
-                    a_push(layer - 1, k).start()
-
             for load in loads(layer, i):
                 load.wait()
 
-            def token_set(k, carry):
-                @pl.when(jnp.logical_and(i >= 1, i <= hn))
+            def token_block(b, carry):
+                k = b // 2
+                at = pl.ds(pl.multiple_of(b % 2 * step, 16), step)
+                rows_b = pl.ds(pl.multiple_of(b * step, 16), step)
+                d_act = mm(gb_cat[rows_b], w2c[i % 2], 1, 1)
+                du = (d_act * gelu_slope(uc[i % 2, k, at].astype(F32))).astype(BF16)
+                du_cat[rows_b, cols(i, chunk)] = du
+
+                @pl.when(jnp.logical_or(layer > 0, k == 0))
                 def _():
-                    du_push(layer, i - 1, k).wait_send()
-
-                def block(b, carry):
-                    at = pl.ds(pl.multiple_of(b * step, 16), step)
-                    rows_b = pl.ds(pl.multiple_of(k * tokens + b * step, 16), step)
-                    d_act = mm(gb_cat[rows_b], w2c[i % 2], 1, 1)
-                    du = (d_act * gelu_slope(uc[i % 2, k, at].astype(F32))).astype(BF16)
-
-                    @pl.when(i < hn)
-                    def _():
-                        du_st[k, at] = du
-
-                    @pl.when(i >= hn)
-                    def _():
-                        du_cat[rows_b, cols(i % hn, chunk)] = du
-
-                    @pl.when(jnp.logical_or(layer > 0, k == 0))
-                    def _():
-                        g[rows_b] += mm(du, w1c[i % 2], 1, 1)
-
-                    return carry
-
-                lax.fori_loop(0, tokens // step, block, 0)
-
-                @pl.when(i < hn)
-                def _():
-                    du_push(layer, i, k).start()
-
-                @pl.when(i >= hn)
-                def _():
-                    du_push(layer, i - hn, k).wait_recv()
-                    du_load(layer, i - hn, k).start()
+                    g[rows_b] += mm(du, w1c[i % 2], 1, 1)
 
                 return carry
 
-            lax.fori_loop(0, 2, token_set, 0)
+            lax.fori_loop(0, 4, token_block, 0)
             return carry
 
         lax.fori_loop(0, nu, first, 0)
         for k in sets:
-            gb_cat[mine(k)] = g[mine(k)].astype(BF16)
+            gb_cat[of(k)] = g[of(k)].astype(BF16)
         for k in sets:
             h_load(layer, k).wait()
-            h_load2(layer, k).wait()
-            for i in range(hn):
-                du_load(layer, i, k).wait()
+
+        @pl.when(layer > 0)
+        def _():
+            for load in loads(layer - 1, 0):
+                load.start()
+            for k in sets:
+                a_load(layer - 1, k).start()
+
+        @pl.when(layer == 0)
+        def _():
+            dx_store().start()
 
         def second(i, carry):
             t = base + nu + i
             mi, fi = i % nm, i // nm
-            out = mm(h_cat[:, cols(mi, part)], du_cat[:, cols(fi, width)], 0, 0)
-            unit[t % SLOTS] = out.reshape(4, rows // 8, width).astype(BF16)
+            lhs = h_cat[:, cols(mi, part)]
+            part0[t % PARTS] = blocks(mm(lhs, du_cat[:, cols((1 - core) * nf + fi, width)], 0, 0))
+            unit[t % SLOTS] = blocks(mm(lhs, du_cat[:, cols(core * nf + fi, width)], 0, 0))
             comm(t)
             push_unit(t)
-
-            @pl.when(layer > 0)
-            def _():
-                @pl.when(i == 0)
-                def _():
-                    for load in loads(layer - 1, 0):
-                        load.start()
-                    for k in sets:
-                        a_push(layer - 1, k).wait()
-                        a_load(layer - 1, k).start()
-                        a_load2(layer - 1, k).start()
-                    for k in sets:
-                        gb_push(layer - 1, k).start()
-
-                @pl.when(i == hn)
-                def _():
-                    for k in sets:
-                        gb_push(layer - 1, k).wait()
-                        gb_load2(layer - 1, k).start()
-
-            @pl.when(jnp.logical_and(layer == 0, i == 0))
-            def _():
-                dx_store().start()
-
             return carry
 
         lax.fori_loop(0, nu, second, 0)
@@ -462,7 +382,7 @@
         comm(t)
         return carry
 
-    lax.fori_loop(units, units + 6 * LAG, drain, 0)
+    lax.fori_loop(units, units + 1 + 5 * LAG + 2, drain, 0)
     dx_store().wait()
 
 
@@ -471,48 +391,37 @@
     tokens = dys[0].shape[0]
     half = wide // 2
     nu = half // rows
-    hn = nu // 2
     chunk = wide // nu
     units = 2 * nu * layers
     dma, reg = pltpu.SemaphoreType.DMA, pltpu.SemaphoreType.REGULAR
     hbm = pl.BlockSpec(memory_space=pl.ANY)
     sub = rows // 8
     shape = jax.ShapeDtypeStruct
-    outs = [
-        shape((units, 2, 8, sub, width), BF16),
-        shape((tokens, width), BF16),
-        shape((layers, 2, tokens, half // 2), BF16),
-        shape((layers, 2, tokens, width // 2), BF16),
-        shape((layers, 2, tokens, half), BF16),
-        shape((layers, 2, tokens, width), BF16),
-    ]
     scratch = [
-        pltpu.VMEM((4 * tokens, half // 2), BF16),
-        pltpu.VMEM((4 * tokens, half), BF16),
-        pltpu.VMEM((4 * tokens, width // 2), BF16),
-        pltpu.VMEM((4 * tokens, width), BF16),
+        pltpu.VMEM((2 * tokens, half), BF16),
+        pltpu.VMEM((2 * tokens, wide), BF16),
+        pltpu.VMEM((2 * tokens, width // 2), BF16),
+        pltpu.VMEM((2 * tokens, width), BF16),
         pltpu.VMEM((2 * tokens, width), F32),
         pltpu.VMEM((2, chunk, width), BF16),
         pltpu.VMEM((2, width, chunk), BF16),
         pltpu.VMEM((2, 2, tokens, chunk), BF16),
-        pltpu.VMEM((2, tokens, chunk), BF16),
         pltpu.VMEM((SLOTS, 4, sub, width), BF16),
+        pltpu.VMEM((PARTS, 4, sub, width), BF16),
+        pltpu.VMEM((RECV0, 4, sub, width), BF16),
         pltpu.VMEM((RECV, 2, sub, width), BF16),
         pltpu.VMEM((RECV, 1, sub, width), BF16),
-        *[dma((SLOTS,))] * 7,
+        *[dma((SLOTS,))] * 11,
         *[dma((RECV,))] * 2,
-        *[dma((SLOTS,))] * 4,
         *[reg((RECV,))] * 2,
-        *[dma((2,))] * 4,
-        dma((2,)), dma((hn, 2)), dma((hn, 2)),
-        *[dma((2,))] * 8,
-        dma((2,)), dma((2,)), dma((2, 2)), dma,
+        dma((PARTS,)), dma((RECV0,)), reg((RECV0,)),
+        dma((2,)), dma((2,)), dma((2,)), dma((2,)), dma((2,)), dma((2, 2)), dma,
     ]
     return pl.pallas_call(
         functools.partial(backward_body, layers=layers, tokens=tokens, width=width, wide=wide, rows=rows),
-        out_shape=outs,
+        out_shape=[shape((units, 2, 8, sub, width), BF16), shape((tokens, width), BF16)],
         in_specs=[hbm] * 10,
-        out_specs=[hbm] * 6,
+        out_specs=[hbm] * 2,
         scratch_shapes=scratch,
         compiler_params=pltpu.CompilerParams(collective_id=0, has_side_effects=True, vmem_limit_bytes=VMEM_LIMIT),
         name="backward",
@@ -593,7 +502,7 @@
         z = jnp.full((1,), lax.axis_index("replica"), jnp.int32)
         kept = [forward(z, tokens, w_one, w_two, rows) for tokens in (x, x_nbr)]
         us, as_, hs = zip(*kept)
-        tot, dx = backward(w_one, w_two, us, as_, hs, (dy, dy_nbr), rows)[:2]
+        tot, dx = backward(w_one, w_two, us, as_, hs, (dy, dy_nbr), rows)
         one, two = assemble(tot, layers, width, wide, rows)
         return one, two, dx.reshape(x_loc.shape)
 

time: 921 us -> 913 us (level)
  no operation moved by 1% of the time
where the time goes in v4:
time: 913 us
  Pallas kernels  906 us (99%)
    pallas_call x1, Pallas kernels, backward(): pl.pallas_call(functools.partial(backward_body, layers=layers, tokens=tok...  640 us
    pallas_call x2, Pallas kernels, forward(): pl.pallas_call(functools.partial(forward_body, layers=layers, chunks=chun...  200 us
    pallas_call x1, Pallas kernels, assemble(): pl.pallas_call(functools.partial(assemble_body, layers=layers, nu=nu, nm=...  67 us
  transfers between devices with their start and end apart: 2, of which 0 were waited for; matrix products, arithmetic and copies ran while one was open for 0% of the time, Pallas kernels for 22%

profile of v4, /device:TPU:0, one launch (start us, length us, event | category | flops | bytes accessed | tf_op | source)
XLA Modules:
  0.0 913.2 jit_solution(14563407605777754825)
XLA Ops:
  0.6 3.3 collective-permute-start
  4.0 0.1 collective-permute-start.1
  4.0 99.8 %forward.2 = (bf16[4,768,5120]{2,1,0:T(8,128)(2,1)}, bf16[4,768,2560]{2,1,0:T(8,128)(2,1)}, bf16[4,768,640]{2,1,0:T(8,128)(2,1)}) custom-call(s32[1]{0:T(128)} %bitcast.z_ref, bf16[768,1280]{1,0:T(8,128)(2,1)} %bitcast.12, bf16[4,1280,5120]{2,1,0:T(8,128)(2,1)} %w1.1, bf16[4,5120,1280]{2,1,0:T(8,128)(2,1)} %w2.1), custom_call_target="tpu_custom_call" | custom-call | flops 70464307200 | bytes 104857600 | tf_op jit(solution)/shard_map/forward/pallas_call | solution.py:76
  103.8 0.0 collective-permute-done.x_ref
  103.8 99.8 %forward.3 = (bf16[4,768,5120]{2,1,0:T(8,128)(2,1)}, bf16[4,768,2560]{2,1,0:T(8,128)(2,1)}, bf16[4,768,640]{2,1,0:T(8,128)(2,1)}) custom-call(s32[1]{0:T(128)} %bitcast.z_ref, bf16[768,1280]{1,0:T(8,128)(2,1)} %collective-permute-done.x_ref, bf16[4,1280,5120]{2,1,0:T(8,128)(2,1)} %w1.1, bf16[4,5120,1280]{2,1,0:T(8,128)(2,1)} %w2.1), custom_call_target="tpu_custom_call" | custom-call | flops 70464307200 | bytes 104857600 | tf_op jit(solution)/shard_map/forward/pallas_call | solution.py:76
  203.6 0.0 collective-permute-done.1.dy_nbr
  203.6 639.6 %backward.1 = (bf16[80,2,8,32,1280]{4,3,2,1,0:T(8,128)(2,1)}, bf16[768,1280]{1,0:T(8,128)(2,1)}) custom-call(bf16[4,1280,5120]{2,1,0:T(8,128)(2,1)} %w1.1, bf16[4,5120,1280]{2,1,0:T(8,128)(2,1)} %w2.1, bf16[4,768,5120]{2,1,0:T(8,128)(2,1)} %get-tuple-element.13.u_own, bf16[4,768,5120]{2,1,0:T(8,128)(2,1)} %get-tuple-element.14.u_nbr, ...), custom_call_target="tpu_custom_call" | custom-call | tf_op jit(solution)/shard_map/backward/pallas_call | solution.py:420
  843.2 67.0 %assemble.1 = (bf16[4,5,8,32,5120]{4,3,2,1,0:T(8,128)(2,1)}, bf16[4,20,8,32,1280]{4,3,2,1,0:T(8,128)(2,1)}) custom-call(bf16[80,2,8,32,1280]{4,3,2,1,0:T(8,128)(2,1)} %get-tuple-element.19.tot), custom_call_target="tpu_custom_call" | custom-call | tf_op jit(solution)/shard_map/assemble/pallas_call | solution.py:480
  910.2 2.9 copy.8
Async XLA Ops:
  0.6 103.2 %collective-permute-start = (bf16[768,1280]{1,0:T(8,128)(2,1)}, bf16[768,1280]{1,0:T(8,128)(2,1)}, u32[]{:S(2)}, u32[]{:S(2)}) collective-permute-start(bf16[768,1280]{1,0:T(8,128)(2,1)} %bitcast.11), channel_id=1, source_target_pairs={{0,8},{8,0},{1,9},{9,1},{2,10},{10,2},{3,11},{11,3},{4,12},{12,4},... | collective-permute-start | bytes 5898248 | tf_op jit(solution)/shard_map/ppermute | solution.py:500
  4.0 199.7 %collective-permute-start.1 = (bf16[768,1280]{1,0:T(8,128)(2,1)}, bf16[768,1280]{1,0:T(8,128)(2,1)}, u32[]{:S(2)}, u32[]{:S(2)}) collective-permute-start(bf16[768,1280]{1,0:T(8,128)(2,1)} %bitcast.6), channel_id=1, source_target_pairs={{0,8},{8,0},{1,9},{9,1},{2,10},{10,2},{3,11},{11,3},{4,12},{12,4},... | collective-permute-start | bytes 5898248 | tf_op jit(solution)/shard_map/ppermute | solution.py:501

commit v5 on v4

--- a/solution.py
+++ b/solution.py
@@ -14,7 +14,8 @@
 C0, C1 = 0.7978845608028654, 0.044715
 UNIT_ROWS = 256
 LAG = 3
-SLOTS, RECV, PARTS, RECV0 = 12, 8, 2, 4
+SLOTS, SEMS, RECV, PARTS, RECV0 = 44, 12, 10, 3, 4
+PACE = 7
 X, Y, Z = 0, 1, 2
 
 
@@ -24,8 +25,8 @@
 
 def gelu_slope(v):
     sq = v * v
-    t = jnp.tanh(C0 * (v + C1 * (sq * v)))
-    return 0.5 * (1.0 + t) + 0.5 * v * (1.0 - t * t) * (C0 * (1.0 + 3.0 * C1 * sq))
+    t = jnp.tanh(v * (C0 + C0 * C1 * sq))
+    return 0.5 + 0.5 * t + v * (1.0 - t * t) * (0.5 * C0 + 1.5 * C0 * C1 * sq)
 
 
 def mm(lhs, rhs, lhs_dim, rhs_dim):
@@ -113,6 +114,8 @@
     nf = nu // nm
     chunk = wide // nu
     units = 2 * nu * layers
+    pieces = 2 * units
+    narrow = width // 2
     step = tokens // 2
     z, rest = lax.axis_index("replica"), lax.axis_index("data")
     core, x, y = rest % 2, (rest // 2) % 2, rest // 4
@@ -130,9 +133,9 @@
     def send(src, dst, ssem, rsem, to):
         return pltpu.make_async_remote_copy(src_ref=src, dst_ref=dst, send_sem=ssem, recv_sem=rsem, device_id=to, device_id_type=MESH)
 
-    def place(n):
-        mid = (n % 3) // 2
-        a_axis = (1 - mid) * (n % 3) + mid * ((n // 3) % 2)
+    def place(m):
+        mid = (m % 3) // 2
+        a_axis = (1 - mid) * (m % 3) + mid * ((m // 3) % 2)
         b_axis = 1 - a_axis
         bit_a = x + a_axis * (y - x)
         bit_b = x + b_axis * (y - x)
@@ -142,43 +145,43 @@
     def rs0(n):
         return send(part0.at[n % PARTS], rcv0.at[n % RECV0], s_rs0.at[n % PARTS], r_rs0.at[n % RECV0], sibling)
 
-    def rs1(n):
-        mid, a_axis, b_axis, bit_a, bit_b, own = place(n)
-        return send(unit.at[n % SLOTS, pl.ds(2 - 2 * bit_a, 2)], rcv1.at[n % RECV], s_rs1.at[n % SLOTS], r_rs1.at[n % RECV], peer(a_axis))
-
-    def rs2(n):
-        mid, a_axis, b_axis, bit_a, bit_b, own = place(n)
-        return send(unit.at[n % SLOTS, pl.ds(2 * bit_a + 1 - bit_b, 1)], rcv2.at[n % RECV], s_rs2.at[n % SLOTS], r_rs2.at[n % RECV], peer(b_axis))
-
-    def own_copy(n):
-        mid, a_axis, b_axis, bit_a, bit_b, own = place(n)
-        return pltpu.make_async_copy(unit.at[n % SLOTS, pl.ds(2 * bit_a + bit_b, 1)], tot.at[n, core, pl.ds(own, 1)], s_own.at[n % SLOTS])
-
-    def ag1(n):
-        mid, a_axis, b_axis, bit_a, bit_b, own = place(n)
+    def rs1(m):
+        mid, a_axis, b_axis, bit_a, bit_b, own = place(m)
+        return send(unit.at[m % SLOTS, pl.ds(2 - 2 * bit_a, 2)], rcv1.at[m % RECV], s_rs1.at[m % SEMS], r_rs1.at[m % RECV], peer(a_axis))
+
+    def rs2(m):
+        mid, a_axis, b_axis, bit_a, bit_b, own = place(m)
+        return send(unit.at[m % SLOTS, pl.ds(2 * bit_a + 1 - bit_b, 1)], rcv2.at[m % RECV], s_rs2.at[m % SEMS], r_rs2.at[m % RECV], peer(b_axis))
+
+    def own_copy(m):
+        mid, a_axis, b_axis, bit_a, bit_b, own = place(m)
+        return pltpu.make_async_copy(unit.at[m % SLOTS, pl.ds(2 * bit_a + bit_b, 1)], tot.at[m, core, pl.ds(own, 1)], s_own.at[m % SEMS])
+
+    def ag1(m):
+        mid, a_axis, b_axis, bit_a, bit_b, own = place(m)
         return send(
-            unit.at[n % SLOTS, pl.ds(2 * bit_a + bit_b, 1)], tot.at[n, core, pl.ds(own, 1)], s_ag1.at[n % SLOTS], r_ag1.at[n % SLOTS], peer(b_axis)
+            unit.at[m % SLOTS, pl.ds(2 * bit_a + bit_b, 1)], tot.at[m, core, pl.ds(own, 1)], s_ag1.at[m % SEMS], r_ag1.at[m % SEMS], peer(b_axis)
         )
 
-    def ag2(n):
-        mid, a_axis, b_axis, bit_a, bit_b, own = place(n)
-        piece = tot.at[n, core, pl.ds(own // 2 * 2, 2)]
-        return send(piece, piece, s_ag2.at[n % SLOTS], r_ag2.at[n % SLOTS], peer(a_axis + mid * (Z - a_axis)))
-
-    def ag3(n):
-        mid, a_axis, b_axis, bit_a, bit_b, own = place(n)
-        piece = tot.at[n, core, pl.ds(own // 4 * 4, 4)]
-        return send(piece, piece, s_ag3.at[n % SLOTS], r_ag3.at[n % SLOTS], peer(Z + mid * (a_axis - Z)))
-
-    def fwd(n):
-        piece = tot.at[n, core]
-        return send(piece, piece, s_fwd.at[n % SLOTS], r_fwd.at[n % SLOTS], sibling)
-
-    def add(n, block, rcv, slot, j):
-        unit[n % SLOTS, block] = (unit[n % SLOTS, block].astype(F32) + rcv[slot, j].astype(F32)).astype(BF16)
-
-    def credit(sem, n, slots, to):
-        @pl.when(n + slots < units)
+    def ag2(m):
+        mid, a_axis, b_axis, bit_a, bit_b, own = place(m)
+        span = tot.at[m, core, pl.ds(own // 2 * 2, 2)]
+        return send(span, span, s_ag2.at[m % SEMS], r_ag2.at[m % SEMS], peer(a_axis + mid * (Z - a_axis)))
+
+    def ag3(m):
+        mid, a_axis, b_axis, bit_a, bit_b, own = place(m)
+        span = tot.at[m, core, pl.ds(own // 4 * 4, 4)]
+        return send(span, span, s_ag3.at[m % SEMS], r_ag3.at[m % SEMS], peer(Z + mid * (a_axis - Z)))
+
+    def fwd(m):
+        span = tot.at[m, core]
+        return send(span, span, s_fwd.at[m % SEMS], r_fwd.at[m % SEMS], sibling)
+
+    def add(m, block, other):
+        unit[m % SLOTS, block] = (unit[m % SLOTS, block].astype(F32) + other.astype(F32)).astype(BF16)
+
+    def credit(sem, n, slots, count, to):
+        @pl.when(n + slots < count)
         def _():
             pl.semaphore_signal(sem.at[n % slots], inc=1, device_id=to, device_id_type=MESH)
 
@@ -187,77 +190,89 @@
         def _():
             pl.semaphore_wait(sem.at[n % slots], 1)
 
-    def live(n):
-        return jnp.logical_and(n >= 0, n < units)
-
-    def comm(t):
-        n0, n1, n2, n3, n4, n5 = (t - 1 - k * LAG for k in range(6))
-        n6 = n5 - 2
-
-        @pl.when(live(n2))
-        def _():
-            mid, a_axis, b_axis, bit_a, bit_b, own = place(n2)
-            rs2(n2).wait_recv()
-            add(n2, 2 * bit_a + bit_b, rcv2, n2 % RECV, 0)
-            credit(c_rs2, n2, RECV, peer(b_axis))
-            rs1(n2).wait_send()
-
-        @pl.when(live(n1))
-        def _():
-            mid, a_axis, b_axis, bit_a, bit_b, own = place(n1)
-            rs1(n1).wait_recv()
-            add(n1, 2 * bit_a + 1 - bit_b, rcv1, n1 % RECV, 1 - bit_b)
-            add(n1, 2 * bit_a + bit_b, rcv1, n1 % RECV, bit_b)
-            credit(c_rs1, n1, RECV, peer(a_axis))
-
-        @pl.when(live(n0))
-        def _():
-            mid, a_axis, b_axis, bit_a, bit_b, own = place(n0)
-            rs0(n0).wait()
-            for first in (2 - 2 * bit_a, 2 * bit_a):
-                for j in range(2):
-                    add(n0, first + j, rcv0, n0 % RECV0, first + j)
-            credit(c_rs0, n0, RECV0, sibling)
-
-        @pl.when(live(n2))
-        def _():
-            own_copy(n2).start()
-            ag1(n2).start()
-
-        @pl.when(live(n1))
-        def _():
-            spend(c_rs2, n1, RECV)
-            rs2(n1).start()
-
-        @pl.when(live(n0))
-        def _():
-            spend(c_rs1, n0, RECV)
-            rs1(n0).start()
-
-        @pl.when(live(n3))
-        def _():
-            rs2(n3).wait_send()
-            own_copy(n3).wait()
-            ag1(n3).wait()
-            ag2(n3).start()
-
-        @pl.when(live(n4))
-        def _():
-            ag2(n4).wait()
-            ag3(n4).start()
-
-        @pl.when(live(n5))
-        def _():
-            ag3(n5).wait()
-            fwd(n5).start()
-
-        @pl.when(live(n6))
-        def _():
-            fwd(n6).wait()
-
-    def push_unit(t):
-        spend(c_rs0, t, RECV0)
-        rs0(t).start()
+    def live(m):
+        return jnp.logical_and(m >= 0, m < pieces)
+
+    def make(n, theirs, mine):
+        part0[n % PARTS] = theirs.reshape(4, rows // 8, width).astype(BF16)
+        kept = mine.reshape(4, rows // 8, width).astype(BF16)
+        for c in range(2):
+            unit[(2 * n + c) % SLOTS] = kept[:, :, c * narrow : (c + 1) * narrow]
+
+    def push(n):
+        spend(c_rs0, n, RECV0)
+        rs0(n).start()
+
+    def pair_sum(n):
+        rs0(n).wait()
+        for c in range(2):
+            for block in range(4):
+                add(2 * n + c, block, rcv0[n % RECV0, block, :, c * narrow : (c + 1) * narrow])
+        credit(c_rs0, n, RECV0, units, sibling)
+
+    def comm(r, carry):
+        m0, m1, m2, m3, m4, m5 = (r - k * LAG for k in range(6))
+        m6 = m5 - LAG
+
+        @pl.when(live(m2))
+        def _():
+            mid, a_axis, b_axis, bit_a, bit_b, own = place(m2)
+            rs2(m2).wait_recv()
+            add(m2, 2 * bit_a + bit_b, rcv2[m2 % RECV, 0])
+            credit(c_rs2, m2, RECV, pieces, peer(b_axis))
+            rs1(m2).wait_send()
+
+        @pl.when(live(m1))
+        def _():
+            mid, a_axis, b_axis, bit_a, bit_b, own = place(m1)
+            rs1(m1).wait_recv()
+            add(m1, 2 * bit_a + 1 - bit_b, rcv1[m1 % RECV, 1 - bit_b])
+            add(m1, 2 * bit_a + bit_b, rcv1[m1 % RECV, bit_b])
+            credit(c_rs1, m1, RECV, pieces, peer(a_axis))
+
+        @pl.when(live(m0))
+        def _():
+            spend(c_rs1, m0, RECV)
+            rs1(m0).start()
+
+        @pl.when(live(m2))
+        def _():
+            own_copy(m2).start()
+            ag1(m2).start()
+
+        @pl.when(live(m1))
+        def _():
+            spend(c_rs2, m1, RECV)
+            rs2(m1).start()
+
+        @pl.when(live(m3))
+        def _():
+            rs2(m3).wait_send()
+            own_copy(m3).wait()
+            ag1(m3).wait()
+            ag2(m3).start()
+
+        @pl.when(live(m4))
+        def _():
+            ag2(m4).wait()
+            ag3(m4).start()
+
+        @pl.when(live(m5))
+        def _():
+            ag3(m5).wait()
+            fwd(m5).start()
+
+        @pl.when(live(m6))
+        def _():
+            fwd(m6).wait()
+
+        return carry
+
+    def rounds(lo, hi):
+        lax.fori_loop(lo, hi, comm, 0)
+
+    def spread(i):
+        return PACE * i * i // (nu * nu)
 
     sets = (0, 1)
     us, as_, hs, dys = (u_own, u_nbr), (a_own, a_nbr), (h_own, h_nbr), (dy_own, dy_nbr)
@@ -287,9 +302,6 @@
 
     def dx_store():
         return pltpu.make_async_copy(gb_cat.at[of(0)], dx, l_dx)
-
-    def blocks(out):
-        return out.reshape(4, rows // 8, width).astype(BF16)
 
     barrier = pltpu.get_barrier_semaphore()
     for to in (peer(X), peer(Y), peer(Z), sibling):
@@ -307,46 +319,63 @@
     def layer_step(li, carry):
         layer = layers - 1 - li
         base = li * 2 * nu
+        late = jnp.minimum(li, 1)
+        r0 = (4 * nu * li - 2 * nu + PACE) * late
+        r1 = r0 + PACE
+        r2 = 4 * nu * li + 2 * nu
         for k in sets:
             a_load(layer, k).wait()
-            h_load(layer, k).start()
-
-        def first(i, carry):
-            t = base + i
+
+        def second_weight(i, carry):
+            n = base + i
             lhs = jnp.concatenate([a_cat[:, cols((1 - core) * nu + i, part)], a_cat[:, cols(core * nu + i, part)]], axis=1)
             out = mm(lhs, gb_cat[...], 0, 0)
-            part0[t % PARTS] = blocks(out[:part])
-            unit[t % SLOTS] = blocks(out[part:])
+            make(n, out[:part], out[part:])
+
+            @pl.when(n >= 2)
+            def _():
+                pair_sum(n - 2)
+
+            push(n)
+            rounds(r0 + spread(i), r0 + spread(i + 1))
+            return carry
+
+        lax.fori_loop(0, nu, second_weight, 0)
+        pair_sum(base + nu - 2)
+        pair_sum(base + nu - 1)
+        for k in sets:
+            h_load(layer, k).start()
+
+        @pl.when(layer > 0)
+        def _():
+            for k in sets:
+                a_load(layer - 1, k).start()
+
+        def hidden_chunk(i, carry):
+            for load in loads(layer, i):
+                load.wait()
 
             @pl.when(i < nu - 1)
             def _():
                 for load in loads(layer, i + 1):
                     load.start()
 
-            comm(t)
-            push_unit(t)
-
-            for load in loads(layer, i):
-                load.wait()
-
-            def token_block(b, carry):
-                k = b // 2
-                at = pl.ds(pl.multiple_of(b % 2 * step, 16), step)
-                rows_b = pl.ds(pl.multiple_of(b * step, 16), step)
-                d_act = mm(gb_cat[rows_b], w2c[i % 2], 1, 1)
-                du = (d_act * gelu_slope(uc[i % 2, k, at].astype(F32))).astype(BF16)
-                du_cat[rows_b, cols(i, chunk)] = du
-
-                @pl.when(jnp.logical_or(layer > 0, k == 0))
-                def _():
-                    g[rows_b] += mm(du, w1c[i % 2], 1, 1)
-
+            def token_set(k, carry):
+                at = [pl.ds(q * step, step) for q in range(2)]
+                rows_q = [pl.ds(pl.multiple_of(k * tokens + q * step, 16), step) for q in range(2)]
+                d_act = [mm(gb_cat[r], w2c[i % 2], 1, 1) for r in rows_q]
+                for q in range(2):
+                    du = (d_act[q] * gelu_slope(uc[i % 2, k, at[q]].astype(F32))).astype(BF16)
+                    du_cat[rows_q[q], cols(i, chunk)] = du
+                    g[rows_q[q]] += mm(du, w1c[i % 2], 1, 1)
+                s = 2 * i + k
+                rounds(r1 + (r2 - r1) * s // (2 * nu), r1 + (r2 - r1) * (s + 1) // (2 * nu))
                 return carry
 
-            lax.fori_loop(0, 4, token_block, 0)
+            lax.fori_loop(0, 2, token_set, 0)
             return carry
 
-        lax.fori_loop(0, nu, first, 0)
+        lax.fori_loop(0, nu, hidden_chunk, 0)
         for k in sets:
             gb_cat[of(k)] = g[of(k)].astype(BF16)
         for k in sets:
@@ -356,33 +385,36 @@
         def _():
             for load in loads(layer - 1, 0):
                 load.start()
-            for k in sets:
-                a_load(layer - 1, k).start()
 
         @pl.when(layer == 0)
         def _():
             dx_store().start()
 
-        def second(i, carry):
-            t = base + nu + i
+        def first_weight(i, carry):
+            n = base + nu + i
             mi, fi = i % nm, i // nm
             lhs = h_cat[:, cols(mi, part)]
-            part0[t % PARTS] = blocks(mm(lhs, du_cat[:, cols((1 - core) * nf + fi, width)], 0, 0))
-            unit[t % SLOTS] = blocks(mm(lhs, du_cat[:, cols(core * nf + fi, width)], 0, 0))
-            comm(t)
-            push_unit(t)
+            make(
+                n,
+                mm(lhs, du_cat[:, cols((1 - core) * nf + fi, width)], 0, 0),
+                mm(lhs, du_cat[:, cols(core * nf + fi, width)], 0, 0),
+            )
+
+            @pl.when(i >= 2)
+            def _():
+                pair_sum(n - 2)
+
+            push(n)
+            rounds(r2 + spread(i), r2 + spread(i + 1))
             return carry
 
-        lax.fori_loop(0, nu, second, 0)
+        lax.fori_loop(0, nu, first_weight, 0)
         return carry
 
     lax.fori_loop(0, layers, layer_step, 0)
-
-    def drain(t, carry):
-        comm(t)
-        return carry
-
-    lax.fori_loop(units, units + 1 + 5 * LAG + 2, drain, 0)
+    pair_sum(units - 2)
+    pair_sum(units - 1)
+    rounds(4 * nu * layers - 2 * nu + PACE, pieces + 6 * LAG)
     dx_store().wait()
 
 
@@ -395,7 +427,7 @@
     units = 2 * nu * layers
     dma, reg = pltpu.SemaphoreType.DMA, pltpu.SemaphoreType.REGULAR
     hbm = pl.BlockSpec(memory_space=pl.ANY)
-    sub = rows // 8
+    sub, narrow = rows // 8, width // 2
     shape = jax.ShapeDtypeStruct
     scratch = [
         pltpu.VMEM((2 * tokens, half), BF16),
@@ -406,12 +438,12 @@
         pltpu.VMEM((2, chunk, width), BF16),
         pltpu.VMEM((2, width, chunk), BF16),
         pltpu.VMEM((2, 2, tokens, chunk), BF16),
-        pltpu.VMEM((SLOTS, 4, sub, width), BF16),
+        pltpu.VMEM((SLOTS, 4, sub, narrow), BF16),
         pltpu.VMEM((PARTS, 4, sub, width), BF16),
         pltpu.VMEM((RECV0, 4, sub, width), BF16),
-        pltpu.VMEM((RECV, 2, sub, width), BF16),
-        pltpu.VMEM((RECV, 1, sub, width), BF16),
-        *[dma((SLOTS,))] * 11,
+        pltpu.VMEM((RECV, 2, sub, narrow), BF16),
+        pltpu.VMEM((RECV, 1, sub, narrow), BF16),
+        *[dma((SEMS,))] * 11,
         *[dma((RECV,))] * 2,
         *[reg((RECV,))] * 2,
         dma((PARTS,)), dma((RECV0,)), reg((RECV0,)),
@@ -419,7 +451,7 @@
     ]
     return pl.pallas_call(
         functools.partial(backward_body, layers=layers, tokens=tokens, width=width, wide=wide, rows=rows),
-        out_shape=[shape((units, 2, 8, sub, width), BF16), shape((tokens, width), BF16)],
+        out_shape=[shape((2 * units, 2, 8, sub, narrow), BF16), shape((tokens, width), BF16)],
         in_specs=[hbm] * 10,
         out_specs=[hbm] * 2,
         scratch_shapes=scratch,
@@ -428,31 +460,34 @@
     )(w_one, w_two, *us, *as_, *hs, *dys)
 
 
-COPY_SLOTS, COPY_LEAD = 24, 10
+COPY_SLOTS, COPY_LEAD = 40, 16
 
 
 def assemble_body(tot, one, two, buf, s_in, s_out, *, layers, nu, nm, width):
-    items = 4 * nu * layers
+    items = 8 * nu * layers
+    narrow = width // 2
 
     def load(j):
         return pltpu.make_async_copy(tot.at[j // 2, j % 2], buf.at[j % COPY_SLOTS], s_in.at[j % COPY_SLOTS])
 
     def stores(j, run):
-        n, core = j // 2, j % 2
-        layer, i, slot = layers - 1 - n // (2 * nu), n % nu, j % COPY_SLOTS
-        mid = (n % 3) // 2
+        m, core, slot = j // 2, j % 2, j % COPY_SLOTS
+        n, side = m // 2, m % 2
+        layer, i = layers - 1 - n // (2 * nu), n % nu
+        mid = (m % 3) // 2
         for q in range(4):
             src = (1 - mid) * q + mid * (q % 2 * 2 + q // 2)
-            piece = buf.at[slot, pl.ds(src * 2, 2)]
+            span = buf.at[slot, pl.ds(src * 2, 2)]
 
             @pl.when((n // nu) % 2 == 0)
             def _():
-                run(pltpu.make_async_copy(piece, two.at[layer, core * nu + i, pl.ds(2 * q, 2)], s_out.at[slot, q]))
+                cols = pl.ds(pl.multiple_of(side * narrow, 128), narrow)
+                run(pltpu.make_async_copy(span, two.at[layer, core * nu + i, pl.ds(2 * q, 2), :, cols], s_out.at[slot, q]))
 
             @pl.when((n // nu) % 2 == 1)
             def _():
-                cols = pl.ds(pl.multiple_of((core * (nu // nm) + i // nm) * width, 128), width)
-                run(pltpu.make_async_copy(piece, one.at[layer, i % nm, pl.ds(2 * q, 2), :, cols], s_out.at[slot, q]))
+                cols = pl.ds(pl.multiple_of((core * (nu // nm) + i // nm) * width + side * narrow, 128), narrow)
+                run(pltpu.make_async_copy(span, one.at[layer, i % nm, pl.ds(2 * q, 2), :, cols], s_out.at[slot, q]))
 
     def step(j, carry):
         @pl.when(j >= COPY_SLOTS)
@@ -482,7 +517,7 @@
         out_shape=[shape((layers, nm, 8, sub, wide), BF16), shape((layers, 2 * nu, 8, sub, width), BF16)],
         in_specs=[hbm],
         out_specs=[hbm, hbm],
-        scratch_shapes=[pltpu.VMEM((COPY_SLOTS, 8, sub, width), BF16), pltpu.SemaphoreType.DMA((COPY_SLOTS,)), pltpu.SemaphoreType.DMA((COPY_SLOTS, 4))],
+        scratch_shapes=[pltpu.VMEM((COPY_SLOTS, 8, sub, width // 2), BF16), pltpu.SemaphoreType.DMA((COPY_SLOTS,)), pltpu.SemaphoreType.DMA((COPY_SLOTS, 4))],
         compiler_params=pltpu.CompilerParams(vmem_limit_bytes=VMEM_LIMIT),
         name="assemble",
     )(tot)

time: 913 us -> 832 us (0.911)
  Pallas kernels: 906 us -> 825 us
    pallas_call x1, Pallas kernels: 640 us -> 557 us  [backward(): pl.pallas_call(functools.partial(backward_body, layers=layers, tokens=tok...]
  transfers between devices with their start and end apart: 2 -> 2, of which waited for: 0 -> 0; matrix products, arithmetic and copies ran while one was open for 0% -> 0% of each run, Pallas kernels for 22% -> 24%
where the time goes in v5:
time: 832 us
  Pallas kernels  825 us (99%)
    pallas_call x1, Pallas kernels, backward(): pl.pallas_call(functools.partial(backward_body, layers=layers, tokens=tok...  557 us
    pallas_call x2, Pallas kernels, forward(): pl.pallas_call(functools.partial(forward_body, layers=layers, chunks=chun...  200 us
    pallas_call x1, Pallas kernels, assemble(): pl.pallas_call(functools.partial(assemble_body, layers=layers, nu=nu, nm=...  68.9 us
  transfers between devices with their start and end apart: 2, of which 0 were waited for; matrix products, arithmetic and copies ran while one was open for 0% of the time, Pallas kernels for 24%

profile of v5, /device:TPU:0, one launch (start us, length us, event | category | flops | bytes accessed | tf_op | source)
XLA Modules:
  0.0 832.0 jit_solution(12850242591719378725)
XLA Ops:
  0.6 3.3 collective-permute-start
  4.0 0.1 collective-permute-start.1
  4.0 99.8 %forward.2 = (bf16[4,768,5120]{2,1,0:T(8,128)(2,1)}, bf16[4,768,2560]{2,1,0:T(8,128)(2,1)}, bf16[4,768,640]{2,1,0:T(8,128)(2,1)}) custom-call(s32[1]{0:T(128)} %bitcast.z_ref, bf16[768,1280]{1,0:T(8,128)(2,1)} %bitcast.12, bf16[4,1280,5120]{2,1,0:T(8,128)(2,1)} %w1.1, bf16[4,5120,1280]{2,1,0:T(8,128)(2,1)} %w2.1), custom_call_target="tpu_custom_call" | custom-call | flops 70464307200 | bytes 104857600 | tf_op jit(solution)/shard_map/forward/pallas_call | solution.py:77
  103.8 0.0 collective-permute-done.x_ref
  103.8 99.8 %forward.3 = (bf16[4,768,5120]{2,1,0:T(8,128)(2,1)}, bf16[4,768,2560]{2,1,0:T(8,128)(2,1)}, bf16[4,768,640]{2,1,0:T(8,128)(2,1)}) custom-call(s32[1]{0:T(128)} %bitcast.z_ref, bf16[768,1280]{1,0:T(8,128)(2,1)} %collective-permute-done.x_ref, bf16[4,1280,5120]{2,1,0:T(8,128)(2,1)} %w1.1, bf16[4,5120,1280]{2,1,0:T(8,128)(2,1)} %w2.1), custom_call_target="tpu_custom_call" | custom-call | flops 70464307200 | bytes 104857600 | tf_op jit(solution)/shard_map/forward/pallas_call | solution.py:77
  203.6 0.0 collective-permute-done.1.dy_nbr
  203.6 556.5 %backward.1 = (bf16[160,2,8,32,640]{4,3,2,1,0:T(8,128)(2,1)}, bf16[768,1280]{1,0:T(8,128)(2,1)}) custom-call(bf16[4,1280,5120]{2,1,0:T(8,128)(2,1)} %w1.1, bf16[4,5120,1280]{2,1,0:T(8,128)(2,1)} %w2.1, bf16[4,768,5120]{2,1,0:T(8,128)(2,1)} %get-tuple-element.13.u_own, bf16[4,768,5120]{2,1,0:T(8,128)(2,1)} %get-tuple-element.14.u_nbr, ...), custom_call_target="tpu_custom_call" | custom-call | tf_op jit(solution)/shard_map/backward/pallas_call | solution.py:452
  760.2 68.9 %assemble.1 = (bf16[4,5,8,32,5120]{4,3,2,1,0:T(8,128)(2,1)}, bf16[4,20,8,32,1280]{4,3,2,1,0:T(8,128)(2,1)}) custom-call(bf16[160,2,8,32,640]{4,3,2,1,0:T(8,128)(2,1)} %get-tuple-element.19.tot), custom_call_target="tpu_custom_call" | custom-call | tf_op jit(solution)/shard_map/assemble/pallas_call | solution.py:515
  829.0 2.9 copy.8
Async XLA Ops:
  0.6 103.2 %collective-permute-start = (bf16[768,1280]{1,0:T(8,128)(2,1)}, bf16[768,1280]{1,0:T(8,128)(2,1)}, u32[]{:S(2)}, u32[]{:S(2)}) collective-permute-start(bf16[768,1280]{1,0:T(8,128)(2,1)} %bitcast.11), channel_id=1, source_target_pairs={{0,8},{8,0},{1,9},{9,1},{2,10},{10,2},{3,11},{11,3},{4,12},{12,4},... | collective-permute-start | bytes 5898248 | tf_op jit(solution)/shard_map/ppermute | solution.py:535
  4.0 199.7 %collective-permute-start.1 = (bf16[768,1280]{1,0:T(8,128)(2,1)}, bf16[768,1280]{1,0:T(8,128)(2,1)}, u32[]{:S(2)}, u32[]{:S(2)}) collective-permute-start(bf16[768,1280]{1,0:T(8,128)(2,1)} %bitcast.6), channel_id=1, source_target_pairs={{0,8},{8,0},{1,9},{9,1},{2,10},{10,2},{3,11},{11,3},{4,12},{12,4},... | collective-permute-start | bytes 5898248 | tf_op jit(solution)/shard_map/ppermute | solution.py:536
